TPU v7x, 32 devices: a 4x4x1 block of a 4x4x8 slice. The times are simulated.
32 devices in a mesh: rep: 2 (over z, core), dp: 16 (over x, y).
Axes of the slice: x: 4, y: 4, z: 1, core: 2. Of those that a mesh axis runs over, the one named last changes fastest.
The devices are a block of a 4x4x8 slice.
Arguments:
- x: bfloat16 [32, 2048, 896], P(('rep', 'dp')), parts along dimension 0
- dy: bfloat16 [32, 2048, 896], P(('rep', 'dp')), parts along dimension 0
- w_gate: bfloat16 [2, 896, 3584], replicated
- w_up: bfloat16 [2, 896, 3584], replicated
- w_down: bfloat16 [2, 3584, 896], replicated
- m_w_gate: float32 [2, 896, 3584], P(None, 'dp')
- m_w_up: float32 [2, 896, 3584], P(None, 'dp')
- m_w_down: float32 [2, 3584, 896], P(None, 'dp')
- v_w_gate: float32 [2, 896, 3584], P(None, 'dp')
- v_w_up: float32 [2, 896, 3584], P(None, 'dp')
- v_w_down: float32 [2, 3584, 896], P(None, 'dp')
Outputs:
- output 1: bfloat16 [4, 896, 3584], P('rep'), parts along dimension 0
- output 2: bfloat16 [4, 896, 3584], P('rep'), parts along dimension 0
- output 3: bfloat16 [4, 3584, 896], P('rep'), parts along dimension 0
- output 4: float32 [4, 896, 3584], P('rep', 'dp'), parts along dimension 0
- output 5: float32 [4, 896, 3584], P('rep', 'dp'), parts along dimension 0
- output 6: float32 [4, 3584, 896], P('rep', 'dp'), parts along dimension 0
- output 7: float32 [4, 896, 3584], P('rep', 'dp'), parts along dimension 0
- output 8: float32 [4, 896, 3584], P('rep', 'dp'), parts along dimension 0
- output 9: float32 [4, 3584, 896], P('rep', 'dp'), parts along dimension 0
There are 2 independent parts. A program takes and returns all parts, laid end to end along the dimension named above; an argument that names none is the same for every part.
All inputs are finite; a program needn't handle non-finite values.
Results may differ from a plain program's by a relative error of at most 0.022.
Values are sent between devices in bfloat16 or wider.
A program may use at most 768 MiB of HBM per device.

v0:
```python
import jax
import jax.numpy as jnp
from jax import lax

NAMES = ("w_gate", "w_up", "w_down")


def matmul(a, w):
    return jnp.dot(a, w, preferred_element_type=jnp.float32).astype(jnp.bfloat16)


def normed(h):
    wide = h.astype(jnp.float32)
    scale = lax.rsqrt(jnp.mean(wide**2, -1, keepdims=True) + 1e-6)
    return (wide * scale).astype(jnp.bfloat16)


def layer(h, w):
    a = normed(h)
    gate = jnp.dot(a, w["w_gate"], preferred_element_type=jnp.float32)
    up = jnp.dot(a, w["w_up"], preferred_element_type=jnp.float32)
    return h + matmul((jax.nn.silu(gate) * up).astype(jnp.bfloat16), w["w_down"])


def adamw(w, m, v, g):
    m = 0.9 * m + 0.1 * g
    v = 0.95 * v + 0.05 * g * g
    step = m * lax.rsqrt(v + 1e-8) + 0.1 * w
    return (w - 0.02 * step).astype(jnp.bfloat16), m, v


def stack(weights, h):
    for number in range(weights["w_gate"].shape[0]):
        h = layer(h, {name: w[number] for name, w in weights.items()})
    return h


def solution(mesh):
    groups = mesh.shape["rep"]

    def step(x, dy, *arrays):
        weights, m, v = (arrays[i : i + 3] for i in (0, 3, 6))
        x, dy = (t.reshape(groups, -1, *t.shape[1:]) for t in (x, dy))

        def of_a_group(x, dy):
            _, back = jax.vjp(lambda w: stack(w, x), dict(zip(NAMES, weights, strict=True)))
            by_weights = back(dy)[0]
            gradients = [by_weights[name].astype(jnp.float32) for name in NAMES]
            new = [adamw(w.astype(jnp.float32), m, v, g) for w, m, v, g in zip(weights, m, v, gradients, strict=True)]
            return tuple(one[which] for which in range(3) for one in new)

        return tuple(t.reshape(-1, *t.shape[2:]) for t in jax.vmap(of_a_group)(x, dy))

    return step
```

profile of v0, /device:TPU:98, one launch (start us, length us, event | category | flops | bytes accessed | tf_op | source)
XLA Modules:
  0.0 1071.3 jit_solution(10695034273156487544)
XLA Ops:
  10.1 6.1 copy
  16.3 23.3 %fusion.67 = f32[2048,3584]{1,0:T(8,128)} fusion(bf16[2,896,3584]{2,1,0:T(8,128)(2,1)} %param, bf16[1,2048,896]{2,1,0:T(8,128)(2,1)} %param.2, f32[2048]{0:T(1024)S(1)} %add_rsqrt_fusion), kind=kOutput, calls=%fused_computation.79 | convolution fusion | flops 13158842368 | bytes 39460864 | tf_op jit(solution)/vmap(jvp())/dot_general | solution.py:20
  39.6 19.1 %fusion.65 = f32[2048,3584]{1,0:T(8,128)} fusion(bf16[2,896,3584]{2,1,0:T(8,128)(2,1)S(1)} %bitcast.346, bf16[1,2048,896]{2,1,0:T(8,128)(2,1)S(1)} %copy-done, f32[2048]{0:T(1024)S(1)} %add_rsqrt_fusion), kind=kOutput, calls=%fused_computation.77 | convolution fusion | flops 13158842368 | bytes 39460864 | tf_op jit(solution)/vmap(jvp())/dot_general | solution.py:21
  58.7 25.8 %fusion.26 = bf16[2048,3584]{1,0:T(8,128)(2,1)} fusion(f32[2048,3584]{1,0:T(8,128)} %fusion.65, f32[2048,3584]{1,0:T(8,128)} %fusion.67), kind=kLoop, calls=%fused_computation.37 | loop fusion | flops 44040192 | bytes 73400320
  84.6 21.5 %fusion.51 = (f32[2048]{0:T(1024)S(1)}, bf16[1,1,2048,896]{2,3,1,0:T(8,128)(2,1)}) fusion(bf16[2048,3584]{1,0:T(8,128)(2,1)} %fusion.26, bf16[2,3584,896]{2,1,0:T(8,128)(2,1)} %param.4, bf16[1,2048,896]{1,2,0:T(8,128)(2,1)} %copy), kind=kOutput, calls=%fused_computation.62 | convolution fusion | flops 13162510336 | bytes 28450816 | tf_op jit(solution)/vmap(jvp())/dot_general | solution.py:9
  106.7 25.0 %fusion.54 = f32[2048,3584]{1,0:T(8,128)} fusion(bf16[2,896,3584]{2,1,0:T(8,128)(2,1)} %param, bf16[1,1,2048,896]{2,3,1,0:T(8,128)(2,1)} %get-tuple-element.10, f32[2048]{0:T(1024)S(1)} %bitcast.348), kind=kOutput, calls=%fused_computation.66 | convolution fusion | flops 13158842368 | bytes 39460864 | tf_op jit(solution)/vmap(jvp())/dot_general | solution.py:20
  131.7 22.2 %fusion.58 = f32[2048,3584]{1,0:T(8,128)} fusion(bf16[2,896,3584]{2,1,0:T(8,128)(2,1)} %param.3, bf16[1,1,2048,896]{2,3,1,0:T(8,128)(2,1)S(1)} %copy-done.4, f32[2048]{0:T(1024)S(1)} %bitcast.349), kind=kOutput, calls=%fused_computation.70 | convolution fusion | flops 13158842368 | bytes 39460864 | tf_op jit(solution)/vmap(jvp())/dot_general | solution.py:21
  153.8 30.0 %fusion.35 = f32[1,3584,896]{2,1,0:T(8,128)} fusion(f32[2048,3584]{1,0:T(8,128)} %fusion.58, f32[2048,3584]{1,0:T(8,128)} %fusion.54, bf16[1,2048,896]{2,1,0:T(8,128)(2,1)S(1)} %copy-done.3), kind=kOutput, calls=%fused_computation.52 | convolution fusion | flops 13197377536 | bytes 75235328 | tf_op jit(solution)/vmap(transpose(jvp()))/dot_general | solution.py:9
  183.9 6.1 copy.1
  190.0 21.9 %convolution_convert_fusion.1 = bf16[2048,3584]{1,0:T(8,128)(2,1)} fusion(bf16[2,3584,896]{2,1,0:T(8,128)(2,1)} %param.4, bf16[1,2048,896]{2,1,0:T(8,128)(2,1)} %param.5), kind=kOutput, calls=%fused_computation.36 | convolution fusion | flops 13160677376 | bytes 24772608 | tf_op jit(solution)/vmap(transpose(jvp()))/dot_general | solution.py:9
  212.0 30.1 %fusion.6 = bf16[2048,3584]{1,0:T(8,128)(2,1)} fusion(f32[2048,3584]{1,0:T(8,128)} %fusion.54, f32[2048,3584]{1,0:T(8,128)} %fusion.58, bf16[2048,3584]{1,0:T(8,128)(2,1)} %convolution_convert_fusion.1), kind=kLoop, calls=%fused_computation.11 | loop fusion | flops 88080384 | bytes 88080384
  242.0 22.4 %fusion.24 = bf16[2048,896]{0,1:T(8,128)(2,1)} fusion(bf16[2048,3584]{1,0:T(8,128)(2,1)} %convolution_convert_fusion.1, f32[2048,3584]{1,0:T(8,128)} %fusion.54, bf16[2,896,3584]{2,1,0:T(8,128)(2,1)} %param.3), kind=kOutput, calls=%fused_computation.34 | convolution fusion | flops 13197377536 | bytes 54132736 | tf_op jit(solution)/vmap(transpose(jvp()))/dot_general | solution.py:21
  264.5 22.1 %fusion.53 = (f32[2048]{0:T(1024)S(1)}, bf16[2048,896]{0,1:T(8,128)(2,1)}) fusion(bf16[1,1,2048,896]{2,3,1,0:T(8,128)(2,1)} %get-tuple-element.10, bf16[2048,896]{0,1:T(8,128)(2,1)} %fusion.24, bf16[2048,3584]{1,0:T(8,128)(2,1)} %fusion.6, bf16[2,896,3584]{2,1,0:T(8,128)(2,1)} %param), kind=kOutput, calls=%fused_computation.64 | convolution fusion | flops 13162510336 | bytes 32120832 | tf_op jit(solution)/vmap(transpose(jvp()))/dot_general | solution.py:20
  286.7 5.8 fusion.81
  294.3 19.8 %convolution_bitcast_fusion = f32[1,3584,896]{2,1,0:T(8,128)} fusion(bf16[2048,3584]{1,0:T(8,128)(2,1)} %fusion.26, bf16[2048,896]{0,1:T(8,128)(2,1)S(1)} %fusion.81), kind=kOutput, calls=%fused_computation.56 | convolution fusion | flops 13153337344 | bytes 31195136 | tf_op jit(solution)/vmap(transpose(jvp()))/dot_general | solution.py:9
  314.2 20.5 %convolution_bitcast_fusion.1 = f32[1,896,3584]{2,1,0:T(8,128)} fusion(bf16[2048,3584]{1,0:T(8,128)(2,1)} %fusion.6, bf16[1,1,2048,896]{2,3,1,0:T(8,128)(2,1)} %get-tuple-element.10, f32[2048]{0:T(1024)S(1)} %bitcast.351), kind=kOutput, calls=%fused_computation.57 | convolution fusion | flops 13158842368 | bytes 31203328 | tf_op jit(solution)/vmap(transpose(jvp()))/dot_general | solution.py:20
  334.9 22.4 %convolution_convert_fusion = bf16[2048,3584]{1,0:T(8,128)(2,1)} fusion(bf16[2048,896]{0,1:T(8,128)(2,1)} %copy-done.5, bf16[2,3584,896]{2,1,0:T(8,128)(2,1)} %param.4), kind=kOutput, calls=%fused_computation.35 | convolution fusion | flops 13160677376 | bytes 24772608 | tf_op jit(solution)/vmap(transpose(jvp()))/dot_general | solution.py:9
  357.3 34.4 %fusion.41 = f32[1,896,3584]{2,1,0:T(8,128)} fusion(f32[2048,3584]{1,0:T(8,128)} %fusion.67, f32[2048,3584]{1,0:T(8,128)} %fusion.65, bf16[2048,3584]{1,0:T(8,128)(2,1)} %convolution_convert_fusion, bf16[1,2048,896]{1,2,0:T(8,128)(2,1)} %copy, f32[2048]{0:T(1024)S(1)} %copy-done.15), kind=kOutput, calls=%fused_computation.54 | convolution fusion | flops 13239582720 | bytes 89923584 | tf_op jit(solution)/vmap(transpose(jvp()))/dot_general | solution.py:20
  391.8 25.9 %fusion.38 = f32[1,896,3584]{2,1,0:T(8,128)} fusion(bf16[2048,3584]{1,0:T(8,128)(2,1)} %convolution_convert_fusion.1, f32[2048,3584]{1,0:T(8,128)} %fusion.54, bf16[1,1,2048,896]{2,3,1,0:T(8,128)(2,1)} %get-tuple-element.10, f32[2048]{0:T(1024)S(1)} %bitcast.352), kind=kOutput, calls=%fused_computation.53 | convolution fusion | flops 13202882560 | bytes 60563456 | tf_op jit(solution)/vmap(transpose(jvp()))/dot_general | solution.py:21
  417.8 25.5 %fusion.44 = f32[1,896,3584]{2,1,0:T(8,128)} fusion(bf16[2048,3584]{1,0:T(8,128)(2,1)} %convolution_convert_fusion, f32[2048,3584]{1,0:T(8,128)} %fusion.67, bf16[1,2048,896]{1,2,0:T(8,128)(2,1)} %copy, f32[2048]{0:T(1024)S(1)} %copy-done.15), kind=kOutput, calls=%fused_computation.55 | convolution fusion | flops 13202882560 | bytes 60563456 | tf_op jit(solution)/vmap(transpose(jvp()))/dot_general | solution.py:21
  448.4 4.1 fusion.121
  452.9 45.6 %reduce-scatter.31.cloned.1.call-done = f32[1,56,3584]{2,1,0:T(8,128)} async-done(((f32[1,896,3584]{2,1,0:T(8,128)}), f32[1,56,3584]{2,1,0:T(8,128)}) %reduce-scatter.31.cloned.1.call-update) | async-done | bytes 802832
  500.4 90.3 %reduce-scatter.33.cloned.1.call-done = f32[1,56,3584]{2,1,0:T(8,128)} async-done(((f32[1,896,3584]{2,1,0:T(8,128)}), f32[1,56,3584]{2,1,0:T(8,128)}) %reduce-scatter.33.cloned.1.call-update) | async-done | bytes 802832
  591.8 5.0 fusion.123
  597.0 85.4 %reduce-scatter.35.cloned.1.call-done = f32[1,56,3584]{2,1,0:T(8,128)} async-done(((f32[1,896,3584]{2,1,0:T(8,128)}), f32[1,56,3584]{2,1,0:T(8,128)}) %reduce-scatter.35.cloned.1.call-update) | async-done | bytes 802832
  684.3 90.3 %reduce-scatter.37.cloned.1.call-done = f32[1,56,3584]{2,1,0:T(8,128)} async-done(((f32[1,896,3584]{2,1,0:T(8,128)}), f32[1,56,3584]{2,1,0:T(8,128)}) %reduce-scatter.37.cloned.1.call-update) | async-done | bytes 802832
  780.0 82.2 %all-gather.14.cloned.1.call-done = bf16[1,2,3584,896]{3,2,1,0:T(8,128)(2,1)} async-done(((bf16[1,2,224,896]{3,2,1,0:T(8,128)(2,1)}), bf16[1,2,3584,896]{3,2,1,0:T(8,128)(2,1)}) %all-gather.14.cloned.1.call-update) | async-done | bytes 12845072 | tf_op jit(solution)/reshape | solution.py:52
  862.2 88.0 %all-gather.10.cloned.1.call-done = bf16[1,2,896,3584]{3,2,1,0:T(8,128)(2,1)} async-done(((bf16[1,2,56,3584]{3,2,1,0:T(8,128)(2,1)}), bf16[1,2,896,3584]{3,2,1,0:T(8,128)(2,1)}) %all-gather.10.cloned.1.call-update) | async-done | bytes 12845072 | tf_op jit(solution)/reshape | solution.py:52
  950.2 88.0 %all-gather.12.cloned.1.call-done = bf16[1,2,896,3584]{3,2,1,0:T(8,128)(2,1)} async-done(((bf16[1,2,56,3584]{3,2,1,0:T(8,128)(2,1)}), bf16[1,2,896,3584]{3,2,1,0:T(8,128)(2,1)}) %all-gather.12.cloned.1.call-update) | async-done | bytes 12845072 | tf_op jit(solution)/reshape | solution.py:52
  1038.2 12.5 %copy.13 = bf16[2,896,3584]{2,1,0:T(8,128)(2,1)} copy(bf16[2,896,3584]{2,1,0:T(8,128)(2,1)} %bitcast.341) | data formatting | bytes 25690112
  1050.7 6.5 copy.14
  1059.7 4.9 copy.15
  (85 shorter events, 23.6 us)
Async XLA Ops:
  7.2 438.1 %reduce-scatter.27.cloned.1.call-start = ((), (), s32[]{:S(2)}) async-start(), calls=%async_computation.9 | async-start | bytes 13647872
  10.1 29.5 %slice-start.4 = ((s8[12845056]{0:T(1024)(128)(4,1)}), s8[262144]{0:T(1024)(128)(4,1)S(1)}, s32[]{:S(2)}) async-start(s8[12845056]{0:T(1024)(128)(4,1)} %bitcast.345), calls=%async_computation.19 | async-start | bytes 524288
  16.2 23.3 %copy-start.14 = (f32[2048]{0:T(1024)}, f32[2048]{0:T(1024)S(1)}, u32[]{:S(2)}) copy-start(f32[2048]{0:T(1024)S(1)} %add_rsqrt_fusion) | copy-start | bytes 24580
  16.3 23.3 %copy-start = (bf16[1,2048,896]{2,1,0:T(8,128)(2,1)S(1)}, bf16[1,2048,896]{2,1,0:T(8,128)(2,1)}, u32[]{:S(2)}) copy-start(bf16[1,2048,896]{2,1,0:T(8,128)(2,1)} %param.2) | copy-start | bytes 11010052
  16.3 23.3 %slice-start.5 = ((s8[12845056]{0:T(1024)(128)(4,1)}), s8[4194304]{0:T(1024)(128)(4,1)S(1)}, s32[]{:S(2)}) async-start(s8[12845056]{0:T(1024)(128)(4,1)} %bitcast.345), calls=%async_computation.20 | async-start | bytes 8388608
  16.3 23.3 %slice-start.6 = ((s8[12845056]{0:T(1024)(128)(4,1)}), s8[4194304]{0:T(1024)(128)(4,1)S(1)}, s32[]{:S(2)}) async-start(s8[12845056]{0:T(1024)(128)(4,1)} %bitcast.345), calls=%async_computation.21 | async-start | bytes 8388608
  16.3 23.3 %slice-start.7 = ((s8[12845056]{0:T(1024)(128)(4,1)}), s8[4194304]{0:T(1024)(128)(4,1)S(1)}, s32[]{:S(2)}) async-start(s8[12845056]{0:T(1024)(128)(4,1)} %bitcast.345), calls=%async_computation.22 | async-start | bytes 8388608
  106.1 25.5 %copy-start.12 = (f32[1,1,2048]{2,1,0:T(1,128)}, f32[1,1,2048]{2,1,0:T(1,128)S(1)}, u32[]{:S(2)}) copy-start(f32[1,1,2048]{2,1,0:T(1,128)S(1)} %rsqrt.31) | copy-start | bytes 24580
  106.7 25.0 %copy-start.4 = (bf16[1,1,2048,896]{2,3,1,0:T(8,128)(2,1)S(1)}, bf16[1,1,2048,896]{2,3,1,0:T(8,128)(2,1)}, u32[]{:S(2)}) copy-start(bf16[1,1,2048,896]{2,3,1,0:T(8,128)(2,1)} %get-tuple-element.10) | copy-start | bytes 11010052
  131.7 22.2 %copy-start.3 = (bf16[1,2048,896]{2,1,0:T(8,128)(2,1)S(1)}, bf16[1,2048,896]{2,1,0:T(8,128)(2,1)}, u32[]{:S(2)}) copy-start(bf16[1,2048,896]{2,1,0:T(8,128)(2,1)} %param.5) | copy-start | bytes 11010052
  183.9 263.3 %reduce-scatter.29.cloned.1.call-start = ((), (), s32[]{:S(2)}) async-start(), calls=%async_computation.10 | async-start | bytes 13647872
  264.5 22.1 %copy-start.11 = (f32[2048]{0:T(1024)S(1)}, f32[2048]{0:T(1024)}, u32[]{:S(2)}) copy-start(f32[2048]{0:T(1024)} %copy-done.10) | copy-start | bytes 24580
  264.5 22.2 %copy-start.1 = (bf16[1,2048,896]{1,2,0:T(8,128)(2,1)S(1)}, bf16[1,2048,896]{1,2,0:T(8,128)(2,1)}, u32[]{:S(2)}) copy-start(bf16[1,2048,896]{1,2,0:T(8,128)(2,1)} %copy.1) | copy-start | bytes 11010052
  264.5 22.2 %copy-start.13 = (f32[1,1,2048]{2,1,0:T(1,128)S(1)}, f32[1,1,2048]{2,1,0:T(1,128)}, u32[]{:S(2)}) copy-start(f32[1,1,2048]{2,1,0:T(1,128)} %copy-done.12) | copy-start | bytes 24580
  292.5 1.8 copy-start.5
  314.2 184.3 %reduce-scatter.31.cloned.1.call-start = ((), (), s32[]{:S(2)}) async-start(), calls=%async_computation.11 | async-start | bytes 13647872
  334.8 22.5 %copy-start.15 = (f32[2048]{0:T(1024)S(1)}, f32[2048]{0:T(1024)}, u32[]{:S(2)}) copy-start(f32[2048]{0:T(1024)} %copy-done.14) | copy-start | bytes 24580
  334.8 255.8 %reduce-scatter.33.cloned.1.call-start = ((), (), s32[]{:S(2)}) async-start(), calls=%async_computation.12 | async-start | bytes 13647872
  391.8 290.6 %reduce-scatter.35.cloned.1.call-start = ((), (), s32[]{:S(2)}) async-start(), calls=%async_computation.13 | async-start | bytes 13647872
  417.8 356.9 %reduce-scatter.37.cloned.1.call-start = ((), (), s32[]{:S(2)}) async-start(), calls=%async_computation.14 | async-start | bytes 13647872
  443.4 5.0 copy-start.6
  443.4 5.0 copy-start.7
  443.4 418.8 %all-gather.14.cloned.1.call-start = ((), (), s32[]{:S(2)}) async-start(), calls=%async_computation.8 | async-start | bytes 13647872 | tf_op jit(solution)/reshape | solution.py:52
  452.6 323.3 %copy-start.8 = (f32[2,56,3584]{2,1,0:T(8,128)S(1)}, f32[2,56,3584]{2,1,0:T(8,128)}, u32[]{:S(2)}) copy-start(f32[2,56,3584]{2,1,0:T(8,128)} %param.8) | copy-start | bytes 4816900
  452.6 323.3 %copy-start.9 = (f32[2,56,3584]{2,1,0:T(8,128)S(1)}, f32[2,56,3584]{2,1,0:T(8,128)}, u32[]{:S(2)}) copy-start(f32[2,56,3584]{2,1,0:T(8,128)} %param.7) | copy-start | bytes 4816900
  452.6 497.6 %all-gather.10.cloned.1.call-start = ((), (), s32[]{:S(2)}) async-start(), calls=%async_computation.6 | async-start | bytes 13647872 | tf_op jit(solution)/reshape | solution.py:52
  596.9 441.3 %all-gather.12.cloned.1.call-start = ((), (), s32[]{:S(2)}) async-start(), calls=%async_computation.7 | async-start | bytes 13647872 | tf_op jit(solution)/reshape | solution.py:52
  1038.2 12.5 %copy-start.2 = (bf16[1,2,896,3584]{3,2,1,0:T(8,128)(2,1)S(1)}, bf16[1,2,896,3584]{3,2,1,0:T(8,128)(2,1)}, u32[]{:S(2)}) copy-start(bf16[1,2,896,3584]{3,2,1,0:T(8,128)(2,1)} %all-gather.12.cloned.1.call-done) | copy-start | bytes 38535172
  1038.2 19.0 %slice-start = ((s8[12845056]{0:T(1024)(128)(4,1)}), s8[4194304]{0:T(1024)(128)(4,1)S(1)}, s32[]{:S(2)}) async-start(s8[12845056]{0:T(1024)(128)(4,1)} %bitcast.338), calls=%async_computation.15 | async-start | bytes 8388608
  1038.2 20.2 %slice-start.1 = ((s8[12845056]{0:T(1024)(128)(4,1)}), s8[4194304]{0:T(1024)(128)(4,1)S(1)}, s32[]{:S(2)}) async-start(s8[12845056]{0:T(1024)(128)(4,1)} %bitcast.338), calls=%async_computation.16 | async-start | bytes 8388608
  1050.7 9.0 slice-start.2
  1050.7 9.0 slice-start.3
  (2 other events, 1.3 us)
Sparse Core Ops, SparseCore 0:
  184.0 91.6 reduce-scatter.26
  314.3 91.6 reduce-scatter.28
  409.8 88.5 reduce-scatter.30
  502.1 88.4 reduce-scatter.32
  593.8 88.5 reduce-scatter.34
  686.1 88.5 reduce-scatter.36
  776.6 85.5 all-gather.13
  864.7 85.4 all-gather.9
  952.8 85.4 all-gather.11
where the time goes:
time: 1080 us; the launch traced here: 1070 us
  waiting for transfers between devices  570 us (53%)
  matrix products  356 us (33%)
  other arithmetic  87.1 us (8%)
  local copies, waits for them, and re-layouts  42.1 us (4%)
  between operations  15 us (1%)
    unnamed x15, waiting for transfers between devices  312 us
    reshape x3, waiting for transfers between devices, step(): t.reshape(-1, *t.shape[2:])  258 us
    dot_general x5, matrix products, layer(): gate = jnp.dot(a, w['w_gate'], preferred_element_type=jnp.float32)  125 us
    dot_general x5, matrix products, matmul(): jnp.dot(a, w, preferred_element_type=jnp.float32).astype(jnp.bfloat16)  116 us
    dot_general x5, matrix products, layer(): up = jnp.dot(a, w['w_up'], preferred_element_type=jnp.float32)  115 us
    unnamed x5, other arithmetic  61.7 us
    unnamed x55, local copies, waits for them, and re-layouts  41.5 us
  transfers between devices with their start and end apart: 9, of which 7 were waited for; matrix products, arithmetic and copies ran while one was open for 26% of the time, Pallas kernels for 0%

commit v1 on v0

v1 whole, which is shorter than its diff:
```python
import functools
import math

import jax
import jax.numpy as jnp
from jax import lax
from jax.experimental import pallas as pl
from jax.experimental.pallas import tpu as pltpu
from jax.sharding import PartitionSpec as P

BLOCK = 256
CHUNKS = 4
LANES = 128
MESH = pl.DeviceIdType.MESH
F32, BF16 = jnp.float32, jnp.bfloat16


def dot(a, b, contract=((1,), (0,))):
    return lax.dot_general(a, b, (contract, ((), ())), preferred_element_type=F32)


def normed(h):
    wide = h.astype(F32)
    scale = lax.rsqrt(jnp.mean(wide**2, -1, keepdims=True) + 1e-6)
    return (wide * scale).astype(BF16)


def adamw(w, m, v, g):
    m = 0.9 * m + 0.1 * g
    v = 0.95 * v + 0.05 * g * g
    step = m * lax.rsqrt(v + 1e-8) + 0.1 * w
    return (w - 0.02 * step).astype(BF16), m, v


def whole(shape):
    return pl.BlockSpec(shape, lambda *_: (0,) * len(shape), pipeline_mode=pl.Buffered(1))


def forward_kernel(x_ref, wg_ref, wu_ref, wd_ref, h_ref, a_ref, acc_ref):
    tokens = x_ref.shape[0]
    chunks, CHUNK = CHUNKS, tokens // CHUNKS
    f = pl.program_id(0)

    @pl.when(f == 0)
    def _():
        @pl.loop(0, chunks)
        def _(c):
            rows = pl.ds(c * CHUNK, CHUNK)
            a_ref[rows] = normed(x_ref[rows])
            acc_ref[rows] = jnp.zeros((CHUNK, x_ref.shape[1]), F32)

    wg, wu, wd = wg_ref[0], wu_ref[0], wd_ref[0]
    for c in range(chunks):
        rows = pl.ds(c * CHUNK, CHUNK)
        a = a_ref[rows]
        gate, up = dot(a, wg), dot(a, wu)
        hidden = (gate * jax.nn.sigmoid(gate) * up).astype(BF16)
        acc_ref[rows] += dot(hidden, wd)

    @pl.when(f == pl.num_programs(0) - 1)
    def _():
        @pl.loop(0, chunks)
        def _(c):
            rows = pl.ds(c * CHUNK, CHUNK)
            h_ref[rows] = x_ref[rows] + acc_ref[rows].astype(BF16)


def forward(x, wg, wu, wd, layer):
    tokens, d = x.shape
    ff = wg.shape[2]
    cost = 6 * tokens * d * ff
    return pl.pallas_call(
        forward_kernel,
        grid=(ff // BLOCK,),
        in_specs=[
            whole((tokens, d)),
            pl.BlockSpec((1, d, BLOCK), lambda f: (layer, 0, f)),
            pl.BlockSpec((1, d, BLOCK), lambda f: (layer, 0, f)),
            pl.BlockSpec((1, BLOCK, d), lambda f: (layer, f, 0)),
        ],
        out_specs=whole((tokens, d)),
        out_shape=jax.ShapeDtypeStruct((tokens, d), BF16),
        scratch_shapes=[pltpu.VMEM((tokens, d), BF16), pltpu.VMEM((tokens, d), F32)],
        cost_estimate=pl.CostEstimate(flops=cost, bytes_accessed=3 * 2 * d * ff, transcendentals=tokens * ff),
        compiler_params=pltpu.CompilerParams(vmem_limit_bytes=60 * 2**20),
        name="forward",
    )(x, wg, wu, wd)


class Ring:
    def __init__(self, side):
        me = lax.axis_index("dp")
        self.side = side
        self.at = (lax.div(me, side), lax.rem(me, side))

    def place(self, axis, offset):
        return lax.rem(self.at[axis] + offset + self.side, self.side)

    def device(self, axis, offset):
        there = [self.at[0], self.at[1]]
        there[axis] = self.place(axis, offset)
        return {"dp": there[0] * self.side + there[1]}

    def meet(self):
        barrier = pltpu.get_barrier_semaphore()
        for axis in range(2):
            for offset in (1, -1):
                pl.semaphore_signal(barrier, inc=1, device_id=self.device(axis, offset), device_id_type=MESH)
        pl.semaphore_wait(barrier, 4)


class Scatter:
    def __init__(self, ring, axis, terms, far, near, sems):
        self.ring, self.axis, self.terms, self.far, self.near, self.sems = ring, axis, terms, far, near, sems

    def copy(self, src, dst, number, offset):
        return pltpu.make_async_remote_copy(
            src_ref=src,
            dst_ref=dst,
            send_sem=self.sems.at[0, number],
            recv_sem=self.sems.at[1, number],
            device_id=self.ring.device(self.axis, offset),
            device_id_type=MESH,
        )

    def first(self, half):
        opposite = self.ring.place(self.axis, 2)
        return self.copy(self.terms.at[opposite, half], self.far.at[half], half, 1 - 2 * half)

    def second(self, side):
        offset = 1 - 2 * side
        return self.copy(self.terms.at[self.ring.place(self.axis, offset)], self.near.at[side], 2 + side, offset)

    def relay(self, own=None):
        for side in range(2):
            self.first(side).wait()
            place = self.ring.place(self.axis, 1 - 2 * side)
            term = self.terms[place, side].astype(F32) if own is None else own(place, side)
            self.terms[place, side] = (term + self.far[side].astype(F32)).astype(BF16)
        for side in range(2):
            self.second(side).start()

    def arrive(self):
        for side in range(2):
            self.second(side).wait()

    def received(self, half):
        return self.near[0, half].astype(F32) + self.near[1, half].astype(F32)


def backward_kernel(side, wanted, h_hbm, dy_ref, *refs):
    wg_refs, wu_refs, wd_refs, refs = refs[:side], refs[side : 2 * side], refs[2 * side : 3 * side], refs[3 * side :]
    gg_ref, gu_ref, gd_ref, h_ref, refs = *refs[:4], refs[4:]
    a_ref, at_ref, dyt_ref, hid_ref, dgate_ref, dup_ref, held_ref, local_sem, refs = *refs[:8], refs[8:]
    ga, gb, gd, ra, rb, rd, na, nb, nd, sa, sb, sd, refs = *refs[:12], refs[12:]
    ha, hb, hd, ra2, rb2, rd2, na2, nb2, nd2, sems, refs = *refs[:10], refs[10:]
    if wanted:
        da_ref = refs[0]
    tokens, d = dy_ref.shape
    size = tokens // CHUNKS
    t, steps = pl.program_id(0), pl.num_programs(0) - 1
    rows = gg_ref.shape[0]
    ring = Ring(side)
    half_d = hd.shape[2]
    first_a, first_b, first_d = (
        Scatter(ring, axis, g, r, n, sems.at[i]) for i, (axis, g, r, n) in enumerate(((0, ga, ra, na), (1, gb, rb, nb), (0, gd, rd, nd)))
    )
    second_a, second_b, second_d = (
        Scatter(ring, axis, g, r, n, sems.at[3 + i])
        for i, (axis, g, r, n) in enumerate(((1, ha, ra2, na2), (0, hb, rb2, nb2), (1, hd, rd2, nd2)))
    )

    @pl.when(t == 0)
    def _():
        ring.meet()
        copy = pltpu.make_async_copy(h_hbm, h_ref, local_sem)
        copy.start()
        copy.wait()
        for c in range(CHUNKS):
            part = pl.ds(c * size, size)
            a = normed(h_ref[part])
            a_ref[part] = a
            at_ref[:, part] = a.T
            dyt_ref[:, part] = dy_ref[part].T
            if wanted:
                da_ref[part] = jnp.zeros((size, d), F32)

    def joined(refs, axis):
        return jnp.concatenate([ref[0] for ref in refs], axis)

    def chunk(c):
        wg, wu, wd = joined(wg_refs, 1), joined(wu_refs, 1), joined(wd_refs, 0)
        part = pl.ds(c * size, size)
        a = a_ref[part]
        gate, up = dot(a, wg), dot(a, wu)
        dhid = dot(dy_ref[part], wd, ((1,), (1,))).astype(BF16).astype(F32)
        s = jax.nn.sigmoid(gate)
        silu = gate * s
        hid_ref[part] = (silu * up).astype(BF16)
        dup = (dhid * silu).astype(BF16)
        dgate = (dhid * up * (s * (1 + gate * (1 - s)))).astype(BF16)
        dup_ref[part] = dup
        dgate_ref[part] = dgate
        if wanted:
            da_ref[part] += dot(dgate, wg, ((1,), (1,))) + dot(dup, wu, ((1,), (1,)))

    def put(g, half):
        for place in range(side):
            ga[place, half] = g[side * rows * place : side * rows * (place + 1), :LANES].astype(BF16)
            mine = [g[rows * (side * x + place) : rows * (side * x + place + 1), LANES:] for x in range(side)]
            gb[place, half] = jnp.concatenate(mine, 0).astype(BF16)

    computing, summing = t < steps, t > 0

    @pl.when(computing)
    def _():
        chunk(0)
        chunk(1)

    @pl.when(summing)
    def _():
        for one in (first_a, first_b, first_d):
            one.relay()

    @pl.when(computing)
    def _():
        chunk(2)
        chunk(3)
        g = dot(dyt_ref[...], hid_ref[...]).T.astype(BF16)
        held_ref[...] = g.reshape(held_ref.shape)

    @pl.when(summing)
    def _():
        for one in (first_a, first_b, first_d):
            one.arrive()
        for one, two, total in ((first_a, second_a, sa), (first_b, second_b, sb)):
            place = ring.place(one.axis, 0)
            for half in range(2):
                value = one.terms[place, half].astype(F32) + one.received(half)
                total[half] = value
                for p in range(side):
                    two.terms[p, half] = value[rows * p : rows * (p + 1)].astype(BF16)
                two.first(half).start()
        place = ring.place(0, 0)
        for half in range(2):
            value = gd[place, half].astype(F32) + first_d.received(half)
            count = value.shape[0]
            sd[pl.ds(pl.multiple_of((2 * (t - 1) + half) * count, count), count)] = value

    @pl.when(computing)
    def _():
        gd[...] = held_ref[...]
        for half in range(2):
            first_d.first(half).start()
        g = dot(at_ref[...], dgate_ref[...])
        put(g, 0)
        first_a.first(0).start()
        first_b.first(0).start()

    def own(total):
        return lambda place, half: total[half, pl.ds(pl.multiple_of(place * rows, 8), rows)]

    @pl.when(summing)
    def _():
        second_a.relay(own(sa))
        second_b.relay(own(sb))

    @pl.when(computing)
    def _():
        g = dot(at_ref[...], dup_ref[...])
        put(g, 1)
        first_a.first(1).start()
        first_b.first(1).start()

    @pl.when(summing)
    def _():
        second_a.arrive()
        second_b.arrive()
        for two, total, tile in ((second_a, sa, 0), (second_b, sb, 1)):
            place = ring.place(two.axis, 0)
            for half, out in enumerate((gg_ref, gu_ref)):
                value = (own(total)(place, half) + two.received(half)).astype(BF16)
                for j in range(value.shape[1] // LANES):
                    lane = pl.multiple_of((t - 1 + steps * (tile + j)) * LANES, LANES)
                    out[:, pl.ds(lane, LANES)] = value[:, j * LANES : (j + 1) * LANES]

    if wanted:

        @pl.when(t == steps - 1)
        def _():
            for c in range(CHUNKS):
                part = pl.ds(c * size, size)
                wide = h_ref[part].astype(F32)
                by_a = da_ref[part].astype(BF16).astype(F32)
                scale = lax.rsqrt(jnp.mean(wide**2, -1, keepdims=True) + 1e-6)
                along = jnp.mean(by_a * wide, -1, keepdims=True)
                by_h = by_a * scale - wide * (along * scale * scale * scale)
                h_ref[part] = dy_ref[part] + by_h.astype(BF16)

    @pl.when(t == steps)
    def _():
        def mine(place, half):
            return sd[pl.ds(pl.multiple_of((2 * place + half) * half_d, 8), half_d)]

        for p in range(side):
            for half in range(2):
                hd[p, half] = mine(p, half).astype(BF16)
        for half in range(2):
            second_d.first(half).start()
        second_d.relay(mine)
        second_d.arrive()
        place = ring.place(1, 0)
        for half in range(2):
            gd_ref[half * half_d : (half + 1) * half_d] = (mine(place, half) + second_d.received(half)).astype(BF16)


def backward(side, h, dy, wg, wu, wd, layer, wanted):
    tokens, d = h.shape
    ff = wg.shape[2]
    tiles = ff // LANES
    steps = tiles // side
    rows, down_rows = d // side**2, ff // side**2
    width = side * LANES

    def tile(j):
        return lambda t: jnp.minimum(t, steps - 1) + steps * j

    across = [pl.BlockSpec((1, d, LANES), lambda t, j=j: (layer, 0, tile(j)(t))) for j in range(side)]
    down = [pl.BlockSpec((1, LANES, d), lambda t, j=j: (layer, tile(j)(t), 0)) for j in range(side)]
    shapes = [(side, 2, side * rows, LANES), (side, 2, side * rows, width - LANES), (side, 2, LANES // 2, d)]
    shapes2 = [(side, 2, rows, LANES), (side, 2, rows, width - LANES), (side, 2, down_rows // 2, d)]

    def buffers(shapes):
        terms = [pltpu.VMEM(s, BF16) for s in shapes]
        far = [pltpu.VMEM(s[1:], BF16) for s in shapes]
        near = [pltpu.VMEM((2, *s[1:]), BF16) for s in shapes]
        return terms + far + near

    totals = [
        pltpu.VMEM((2, side * rows, LANES), F32),
        pltpu.VMEM((2, side * rows, width - LANES), F32),
        pltpu.VMEM((side * down_rows, d), F32),
    ]
    scratch = [
        pltpu.VMEM((tokens, d), BF16),
        pltpu.VMEM((d, tokens), BF16),
        pltpu.VMEM((d, tokens), BF16),
        pltpu.VMEM((tokens, width), BF16),
        pltpu.VMEM((tokens, width), BF16),
        pltpu.VMEM((tokens, width), BF16),
        pltpu.VMEM(shapes[2], BF16),
        pltpu.SemaphoreType.DMA,
        *buffers(shapes),
        *totals,
        *buffers(shapes2),
        pltpu.SemaphoreType.DMA((6, 2, 4)),
    ]
    out_specs = [whole((rows, ff)), whole((rows, ff)), whole((down_rows, d)), whole((tokens, d))]
    out_shape = [jax.ShapeDtypeStruct(s, BF16) for s in ((rows, ff), (rows, ff), (down_rows, d), (tokens, d))]
    if wanted:
        scratch.append(pltpu.VMEM((tokens, d), F32))
    return pl.pallas_call(
        functools.partial(backward_kernel, side, wanted),
        grid=(steps + 1,),
        in_specs=[pl.BlockSpec(memory_space=pl.ANY), whole((tokens, d)), *across, *across, *down],
        out_specs=out_specs,
        out_shape=out_shape,
        scratch_shapes=scratch,
        cost_estimate=pl.CostEstimate(
            flops=2 * tokens * d * ff * (8 if wanted else 6), bytes_accessed=6 * 2 * d * ff, transcendentals=tokens * ff
        ),
        compiler_params=pltpu.CompilerParams(vmem_limit_bytes=63 * 2**20, collective_id=1 + layer, has_side_effects=True),
        name=f"backward_{layer}",
    )(h, dy, *[wg] * side, *[wu] * side, *[wd] * side)


def gather_kernel(side, *refs):
    count = len(refs) // 2 - 1
    shards, outs, (sems, local_sems) = refs[:count], refs[count : 2 * count], refs[2 * count :]
    ring = Ring(side)
    ring.meet()
    units = [(i, n) for n in reversed(range(shards[0].shape[0])) for i in range(count)]
    me = ring.at[0] * side + ring.at[1]

    def rows_of(i, first, many=1):
        rows = shards[i].shape[1]
        return pl.ds(pl.multiple_of(first * rows, 8), many * rows)

    def halves(ref, i, n, first, many, half):
        rows, columns = shards[i].shape[1:]
        if columns % (2 * LANES) == 0:
            return ref.at[n, rows_of(i, first, many), pl.ds(half * (columns // 2), columns // 2)]
        length = many * rows // 2
        return ref.at[n, pl.ds(pl.multiple_of(first * rows + half * length, 8), length)]

    class Phase:
        def __init__(self, number, i, n, axis, first, many, src):
            self.number, self.i, self.n, self.axis, self.first, self.many, self.src = number, i, n, axis, first, many, src

        def copy(self, src, dst, which, offset):
            return pltpu.make_async_remote_copy(
                src_ref=src,
                dst_ref=dst,
                send_sem=sems.at[0, self.number, which],
                recv_sem=sems.at[1, self.number, which],
                device_id=ring.device(self.axis, offset),
                device_id_type=MESH,
            )

        def near(self, side):
            dst = outs[self.i].at[self.n, rows_of(self.i, self.first(0), self.many)]
            return self.copy(dst if self.src is None else self.src, dst, side, 1 - 2 * side)

        def far(self, side):
            offset = 1 - 2 * side
            part = halves(outs[self.i], self.i, self.n, self.first(-offset), self.many, side)
            return self.copy(part, part, 2 + side, offset)

        def start(self):
            for side in range(2):
                self.near(side).start()

        def relay(self):
            for side in range(2):
                self.near(side).wait_recv()
                self.far(side).start()

        def arrive(self):
            for side in range(2):
                self.far(side).wait_recv()

        def finish(self):
            for side in range(2):
                self.near(side).wait_send()
                self.far(side).wait_send()

    one, two, number = {}, {}, 0
    for i, n in units:
        own = shards[i].at[n]
        if n % 2:
            one[i, n] = Phase(number, i, n, 1, lambda o: ring.at[0] * side + ring.place(1, o), 1, own)
            two[i, n] = [Phase(number + 1, i, n, 0, lambda o: ring.place(0, o) * side, side, None)]
        else:
            one[i, n] = Phase(number, i, n, 0, lambda o: ring.place(0, o) * side + ring.at[1], 1, own)
            two[i, n] = [
                Phase(number + 1 + k, i, n, 1, lambda o, k=k: k * side + ring.place(1, o), 1, None) for k in range(side)
            ]
        number += 1 + len(two[i, n])

    def local(i, n):
        return pltpu.make_async_copy(shards[i].at[n], outs[i].at[n, rows_of(i, me)], local_sems.at[i, n])

    for unit in units:
        one[unit].start()
        local(*unit).start()
    for unit in units:
        one[unit].relay()
    for unit in units:
        one[unit].arrive()
        local(*unit).wait()
        for phase in two[unit]:
            phase.start()
    for unit in units:
        for phase in two[unit]:
            phase.relay()
    for unit in units:
        for phase in two[unit]:
            phase.arrive()
    for unit in units:
        for phase in (one[unit], *two[unit]):
            phase.finish()


def gather(side, shards):
    layers = shards[0].shape[0]
    phases = len(shards) * sum(2 if n % 2 else 1 + side for n in range(layers))
    return pl.pallas_call(
        functools.partial(gather_kernel, side),
        in_specs=[pl.BlockSpec(memory_space=pltpu.VMEM)] * len(shards),
        out_specs=[pl.BlockSpec(memory_space=pl.ANY)] * len(shards),
        out_shape=[jax.ShapeDtypeStruct((layers, s.shape[1] * side**2, s.shape[2]), s.dtype) for s in shards],
        scratch_shapes=[
            pltpu.SemaphoreType.DMA((2, phases, 4)),
            pltpu.SemaphoreType.DMA((len(shards), layers)),
        ],
        compiler_params=pltpu.CompilerParams(vmem_limit_bytes=60 * 2**20, collective_id=0, has_side_effects=True),
        name="gather",
    )(*shards)


def solution(mesh):
    side = math.isqrt(mesh.shape["dp"])

    def step(x, dy, *arrays):
        weights, ms, vs = (arrays[i : i + 3] for i in (0, 3, 6))
        x, dy = x[0], dy[0]
        layers = weights[0].shape[0]
        me = lax.axis_index("dp")

        states = [x]
        for n in range(layers - 1):
            states.append(forward(states[-1], *weights, n))

        grads = [None] * layers
        for n in reversed(range(layers)):
            *grads[n], dy = backward(side, states[n], dy, *weights, n, n > 0)
        new = []
        for which in range(3):
            w, m, v = weights[which], ms[which], vs[which]
            rows = m.shape[1]
            mine = lax.dynamic_slice_in_dim(w, me * rows, rows, 1)
            g = jnp.stack([grads[n][which] for n in range(layers)])
            new.append(adamw(mine.astype(F32), m, v, g.astype(F32)))
        gathered = gather(side, [one[0] for one in new])
        return (*gathered, *(one[1] for one in new), *(one[2] for one in new))

    tokens, row = P(("rep", "dp"), None, None), P(None, "dp", None)
    return jax.shard_map(
        step,
        mesh=mesh,
        in_specs=(tokens,) * 2 + (P(),) * 3 + (row,) * 6,
        out_specs=(P("rep", None, None),) * 3 + (P("rep", "dp", None),) * 6,
        check_vma=False,
    )
```

time: 1080 us -> 694 us (0.64)
  Pallas kernels: 0 us -> 653 us
  waiting for transfers between devices: 570 us -> 0 us
  matrix products: 356 us -> 0 us
  other arithmetic: 87.1 us -> 9.54 us
  local copies, waits for them, and re-layouts: 42.1 us -> 27.5 us
  between operations: 15 us -> 1.02 us
    pallas_call x0 -> x4, Pallas kernels: none -> 653 us  [the longest x2 414 us: backward(): pl.pallas_call(functools.partial(backward_kernel, side, wanted), grid=(st...]
    dot_general x15 -> x0, matrix products: 356 us -> none  [the longest x5 125 us: layer(): gate = jnp.dot(a, w['w_gate'], preferred_element_type=jnp.float32)]
    unnamed x15 -> x0, waiting for transfers between devices: 312 us -> none
    reshape x3 -> x0, waiting for transfers between devices: 258 us -> none  [step(): t.reshape(-1, *t.shape[2:])]
    unnamed x5 -> x1, other arithmetic: 61.7 us -> 0.01 us
    unnamed x55 -> x31, local copies, waits for them, and re-layouts: 41.5 us -> 27.5 us
    reshape x3 -> x0, other arithmetic: 13.2 us -> none  [step(): t.reshape(-1, *t.shape[2:])]
  transfers between devices with their start and end apart: 9 -> 0, of which waited for: 7 -> 0; matrix products, arithmetic and copies ran while one was open for 26% -> 0% of each run, Pallas kernels for 0% -> 0%
where the time goes in v1:
time: 694 us; the launch traced here: 691 us
  Pallas kernels  653 us (94%)
  local copies, waits for them, and re-layouts  27.5 us (4%)
  other arithmetic  9.54 us (1%)
    pallas_call x2, Pallas kernels, backward(): pl.pallas_call(functools.partial(backward_kernel, side, wanted), grid=(st...  414 us
    pallas_call x1, Pallas kernels, gather(): pl.pallas_call(functools.partial(gather_kernel, side), in_specs=[pl.Block...  183 us
    pallas_call x1, Pallas kernels, forward(): pl.pallas_call(forward_kernel, grid=(ff // BLOCK,), in_specs=[whole((toke...  55.1 us
    unnamed x31, local copies, waits for them, and re-layouts  27.5 us

profile of v1, /device:TPU:98, one launch (start us, length us, event | category | flops | bytes accessed | tf_op | source)
XLA Modules:
  0.0 690.7 jit_solution(4024621227405322800)
XLA Ops:
  0.6 55.1 %forward.1.h_hbm = bf16[2048,896]{1,0:T(8,128)(2,1)} custom-call(bf16[2048,896]{1,0:T(8,128)(2,1)} %bitcast.17, bf16[2,896,3584]{2,1,0:T(8,128)(2,1)} %refs_3_.3, bf16[2,896,3584]{2,1,0:T(8,128)(2,1)} %refs_7_.3, bf16[2,3584,896]{2,1,0:T(8,128)(2,1)} %refs_11_.3), custom_call_target="tpu_custom_call" | custom-call | flops 39460012032 | bytes 19267584 | tf_op jit(solution)/shard_map/forward/pallas_call | solution.py:72
  55.7 221.1 %backward_1.1 = (bf16[56,3584]{1,0:T(8,128)(2,1)}, bf16[56,3584]{1,0:T(8,128)(2,1)}, bf16[224,896]{1,0:T(8,128)(2,1)}, bf16[2048,896]{1,0:T(8,128)(2,1)}) custom-call(bf16[2048,896]{1,0:T(8,128)(2,1)} %forward.1.h_hbm, bf16[2048,896]{1,0:T(8,128)(2,1)} %bitcast.16, bf16[2,896,3584]{2,1,0:T(8,128)(2,1)} %refs_3_.3, bf16[2,896,3584]{2,1,0:T(8,128)(2,1)} %refs_3_.3, ...), custom_call_target="tpu_custom_call" | custom-call | flops 105226698752 | bytes 38535168 | tf_op jit(solution)/shard_map/backward_1/pallas_call | solution.py:362
  276.8 0.0 copy-start.9
  276.8 193.1 %backward_0.1 = (bf16[56,3584]{1,0:T(8,128)(2,1)}, bf16[56,3584]{1,0:T(8,128)(2,1)}, bf16[224,896]{1,0:T(8,128)(2,1)}, bf16[2048,896]{1,0:T(8,128)(2,1)}) custom-call(bf16[2048,896]{1,0:T(8,128)(2,1)} %bitcast.18, bf16[2048,896]{1,0:T(8,128)(2,1)} %get-tuple-element.19.dy_ref, bf16[2,896,3584]{2,1,0:T(8,128)(2,1)} %refs_3_.3, bf16[2,896,3584]{2,1,0:T(8,128)(2,1)} %refs_3_.3, ...), custom_call_target="tpu_custom_call" | custom-call | flops 78920024064 | bytes 38535168 | tf_op jit(solution)/shard_map/backward_0/pallas_call | solution.py:362
  470.0 0.0 copy-done.9
  470.0 0.0 copy-start.1
  470.0 0.0 copy-start.2
  470.0 0.0 copy-start.3
  470.0 0.0 copy-start.4
  470.0 0.0 copy-start.5
  470.0 0.0 copy-start.6
  470.0 0.0 copy-start.7
  470.0 0.0 copy-start.8
  470.1 4.8 fusion.10
  474.8 0.0 copy-done.1
  474.9 0.0 copy-done.3
  474.9 0.3 copy-done.4
  475.2 0.3 copy-done.5
  475.5 0.3 copy-done.6
  475.8 0.1 copy-done.7
  475.9 0.1 copy-done.8
  476.0 4.7 fusion.2
  480.7 183.3 %gather.1 = (bf16[2,896,3584]{2,1,0:T(8,128)(2,1)}, bf16[2,896,3584]{2,1,0:T(8,128)(2,1)}, bf16[2,3584,896]{2,1,0:T(8,128)(2,1)}) custom-call(bf16[2,56,3584]{2,1,0:T(8,128)(2,1)} %get-tuple-element.35.refs_0_, bf16[2,56,3584]{2,1,0:T(8,128)(2,1)} %get-tuple-element.38.refs_1_, bf16[2,224,896]{2,1,0:T(8,128)(2,1)} %get-tuple-element.29.refs_2_), custom_call_target="tpu_custom_call" | custom-call | tf_op jit(solution)/shard_map/gather/pallas_call | solution.py:477
  664.1 0.0 slice-start
  664.1 0.0 slice-start.1
  664.1 12.5 %copy.23 = bf16[2,896,3584]{2,1,0:T(8,128)(2,1)} copy(bf16[2,896,3584]{2,1,0:T(8,128)(2,1)} %get-tuple-element.50) | data formatting | bytes 25690112
  676.6 0.0 copy-done
  676.6 6.5 copy.24
  683.2 0.0 slice-done
  683.2 1.1 slice-done.1
  684.3 1.3 slice-done.2
  685.6 4.9 copy.25
  (6 shorter events, 0.0 us)
Async XLA Ops:
  276.8 193.1 %copy-start.9 = (bf16[224,896]{1,0:T(8,128)(2,1)S(1)}, bf16[224,896]{1,0:T(8,128)(2,1)}, u32[]{:S(2)}) copy-start(bf16[224,896]{1,0:T(8,128)(2,1)} %get-tuple-element.25) | copy-start | bytes 1204228
  470.0 4.9 copy-start.1
  470.0 4.9 copy-start.2
  470.0 4.9 copy-start.3
  470.0 5.2 copy-start.4
  470.0 5.5 copy-start.5
  470.0 5.7 copy-start.6
  470.0 5.8 copy-start.7
  470.0 6.0 copy-start.8
  664.1 12.5 %copy-start = (bf16[2,896,3584]{2,1,0:T(8,128)(2,1)S(1)}, bf16[2,896,3584]{2,1,0:T(8,128)(2,1)}, u32[]{:S(2)}) copy-start(bf16[2,896,3584]{2,1,0:T(8,128)(2,1)} %get-tuple-element.51) | copy-start | bytes 38535172
  664.1 19.0 %slice-start = ((s8[12845056]{0:T(1024)(128)(4,1)}), s8[4194304]{0:T(1024)(128)(4,1)S(1)}, s32[]{:S(2)}) async-start(s8[12845056]{0:T(1024)(128)(4,1)} %bitcast.8), calls=%async_computation | async-start | bytes 8388608
  664.1 20.2 %slice-start.1 = ((s8[12845056]{0:T(1024)(128)(4,1)}), s8[4194304]{0:T(1024)(128)(4,1)S(1)}, s32[]{:S(2)}) async-start(s8[12845056]{0:T(1024)(128)(4,1)} %bitcast.8), calls=%async_computation.1 | async-start | bytes 8388608
  676.6 8.9 %slice-start.2 = ((s8[12845056]{0:T(1024)(128)(4,1)}), s8[4194304]{0:T(1024)(128)(4,1)S(1)}, s32[]{:S(2)}) async-start(s8[12845056]{0:T(1024)(128)(4,1)} %bitcast.8), calls=%async_computation.2 | async-start | bytes 8388608
  676.6 8.9 %slice-start.3 = ((s8[12845056]{0:T(1024)(128)(4,1)}), s8[262144]{0:T(1024)(128)(4,1)S(1)}, s32[]{:S(2)}) async-start(s8[12845056]{0:T(1024)(128)(4,1)} %bitcast.8), calls=%async_computation.3 | async-start | bytes 524288

commit v2 on v1

--- a/solution.py
+++ b/solution.py
@@ -148,14 +148,141 @@
         return self.near[0, half].astype(F32) + self.near[1, half].astype(F32)
 
 
-def backward_kernel(side, wanted, h_hbm, dy_ref, *refs):
+class Piece:
+    def __init__(self, ring, axis, src, block, part, sems, number):
+        self.ring, self.axis, self.src, self.block, self.part, self.sems, self.number = ring, axis, src, block, part, sems, number
+
+    def copy(self, src, dst, which, offset):
+        return pltpu.make_async_remote_copy(
+            src_ref=src,
+            dst_ref=dst,
+            send_sem=self.sems.at[0, self.number, which],
+            recv_sem=self.sems.at[1, self.number, which],
+            device_id=self.ring.device(self.axis, offset),
+            device_id_type=MESH,
+        )
+
+    def near(self, side):
+        return self.copy(self.block(0) if self.src is None else self.src, self.block(0), side, 1 - 2 * side)
+
+    def far(self, side):
+        offset = 1 - 2 * side
+        return self.copy(self.part(-offset, side), self.part(-offset, side), 2 + side, offset)
+
+    def start(self):
+        for side in range(2):
+            self.near(side).start()
+
+    def relay(self):
+        for side in range(2):
+            self.near(side).wait_recv()
+            self.far(side).start()
+
+    def arrive(self):
+        for side in range(2):
+            self.far(side).wait_recv()
+
+    def sent(self):
+        for side in range(2):
+            self.near(side).wait_send()
+            self.far(side).wait_send()
+
+
+class Gather:
+    def __init__(self, ring, shards, outs, layer, sems, local_sems):
+        self.ring, self.shards, self.outs, self.layer, self.local_sems = ring, shards, outs, layer, local_sems
+        side = ring.side
+        self.ones, self.pairs = [], []
+        for i in range(3):
+            pair = [[] for _ in range(side)]
+            for half in range(2):
+                axis = 1 - half
+                unit = 2 * i + half
+
+                def owner(offset, axis=axis):
+                    at = [ring.at[0], ring.at[1]]
+                    at[axis] = ring.place(axis, offset)
+                    return at[0] * side + at[1]
+
+                self.ones.append(self.piece(i, half, axis, owner, self.region(shards[i], i, 0, half), sems, unit))
+                for k in range(side):
+
+                    def owner(offset, axis=axis, k=k):
+                        at = [k, k]
+                        at[1 - axis] = ring.place(1 - axis, offset)
+                        return at[0] * side + at[1]
+
+                    pair[k].append(self.piece(i, half, 1 - axis, owner, None, sems, 6 + unit * side + k))
+            self.pairs += pair
+
+    def piece(self, i, half, axis, owner, src, sems, number):
+        out = self.outs[i].at[self.layer]
+        return Piece(
+            self.ring,
+            axis,
+            src,
+            lambda offset: self.region(out, i, owner(offset), half),
+            lambda offset, part: self.region(out, i, owner(offset), half, part),
+            sems,
+            number,
+        )
+
+    def region(self, ref, i, owner, half, part=None):
+        rows, columns = self.shards[i].shape
+        share = 2 if part is None else 4
+        which = half if part is None else 2 * half + part
+        if columns % (4 * LANES) == 0:
+            first = owner * rows
+            return ref.at[pl.ds(pl.multiple_of(first, 8), rows), pl.ds(which * (columns // share), columns // share)]
+        length = rows // share
+        return ref.at[pl.ds(pl.multiple_of(owner * rows + which * length, 8), length)]
+
+    def local(self, i):
+        rows = self.shards[i].shape[0]
+        me = self.ring.at[0] * self.ring.side + self.ring.at[1]
+        out = self.outs[i].at[self.layer, pl.ds(pl.multiple_of(me * rows, 8), rows)]
+        return pltpu.make_async_copy(self.shards[i], out, self.local_sems.at[i])
+
+    def start(self):
+        for one in self.ones:
+            one.start()
+        for i in range(3):
+            self.local(i).start()
+
+    def relay(self):
+        for one in self.ones:
+            one.relay()
+
+    def arrive(self):
+        for one in self.ones:
+            one.arrive()
+        for i in range(3):
+            self.local(i).wait()
+
+    def finish(self):
+        for pair in self.pairs:
+            for piece in pair:
+                piece.arrive()
+        for one in (*self.ones, *(piece for pair in self.pairs for piece in pair)):
+            one.sent()
+
+
+def backward_kernel(side, wanted, gathered, h_hbm, dy_ref, *refs):
     wg_refs, wu_refs, wd_refs, refs = refs[:side], refs[side : 2 * side], refs[2 * side : 3 * side], refs[3 * side :]
-    gg_ref, gu_ref, gd_ref, h_ref, refs = *refs[:4], refs[4:]
+    if gathered is not None:
+        shards, refs = refs[:3], refs[3:]
+    gg_ref, gu_ref, gd_ref, *refs = refs
+    if wanted:
+        h_ref, *refs = refs
+    if gathered is not None:
+        outs, refs = refs[:3], refs[3:]
     a_ref, at_ref, dyt_ref, hid_ref, dgate_ref, dup_ref, held_ref, local_sem, refs = *refs[:8], refs[8:]
     ga, gb, gd, ra, rb, rd, na, nb, nd, sa, sb, sd, refs = *refs[:12], refs[12:]
     ha, hb, hd, ra2, rb2, rd2, na2, nb2, nd2, sems, refs = *refs[:10], refs[10:]
     if wanted:
-        da_ref = refs[0]
+        da_ref, *refs = refs
+    else:
+        h_ref, *refs = refs
     tokens, d = dy_ref.shape
     size = tokens // CHUNKS
     t, steps = pl.program_id(0), pl.num_programs(0) - 1
@@ -170,9 +297,32 @@
         for i, (axis, g, r, n) in enumerate(((1, ha, ra2, na2), (0, hb, rb2, nb2), (1, hd, rd2, nd2)))
     )
 
+    if gathered is not None:
+        others = Gather(ring, shards, outs, gathered, *refs)
+
+    def beside(second):
+        if gathered is None:
+            return
+        many = -(-len(others.pairs) // (pl.num_programs(0) - 2))
+        for number, pair in enumerate(others.pairs):
+            when, late = 1 + number // many, number % many >= (many + 1) // 2
+            if late == second:
+
+                @pl.when(t == when)
+                def _(pair=pair):
+                    for piece in pair:
+                        piece.start()
+
+                @pl.when(t == when + 1)
+                def _(pair=pair):
+                    for piece in pair:
+                        piece.relay()
+
     @pl.when(t == 0)
     def _():
         ring.meet()
+        if gathered is not None:
+            others.start()
         copy = pltpu.make_async_copy(h_hbm, h_ref, local_sem)
         copy.start()
         copy.wait()
@@ -222,12 +372,26 @@
         for one in (first_a, first_b, first_d):
             one.relay()
 
+    if gathered is not None:
+
+        @pl.when(t == 1)
+        def _():
+            others.arrive()
+
+    beside(False)
+
     @pl.when(computing)
     def _():
         chunk(2)
         chunk(3)
         g = dot(dyt_ref[...], hid_ref[...]).T.astype(BF16)
         held_ref[...] = g.reshape(held_ref.shape)
+
+    if gathered is not None:
+
+        @pl.when(t == 0)
+        def _():
+            others.relay()
 
     @pl.when(summing)
     def _():
@@ -247,6 +411,17 @@
             count = value.shape[0]
             sd[pl.ds(pl.multiple_of((2 * (t - 1) + half) * count, count), count)] = value
 
+    def mine(place, half):
+        return sd[pl.ds(pl.multiple_of((2 * place + half) * half_d, 8), half_d)]
+
+    @pl.when(t == steps)
+    def _():
+        for p in range(side):
+            for half in range(2):
+                hd[p, half] = mine(p, half).astype(BF16)
+        for half in range(2):
+            second_d.first(half).start()
+
     @pl.when(computing)
     def _():
         gd[...] = held_ref[...]
@@ -264,6 +439,12 @@
     def _():
         second_a.relay(own(sa))
         second_b.relay(own(sb))
+
+    @pl.when(t == steps)
+    def _():
+        second_d.relay(mine)
+
+    beside(True)
 
     @pl.when(computing)
     def _():
@@ -299,22 +480,15 @@
 
     @pl.when(t == steps)
     def _():
-        def mine(place, half):
-            return sd[pl.ds(pl.multiple_of((2 * place + half) * half_d, 8), half_d)]
-
-        for p in range(side):
-            for half in range(2):
-                hd[p, half] = mine(p, half).astype(BF16)
-        for half in range(2):
-            second_d.first(half).start()
-        second_d.relay(mine)
         second_d.arrive()
         place = ring.place(1, 0)
         for half in range(2):
             gd_ref[half * half_d : (half + 1) * half_d] = (mine(place, half) + second_d.received(half)).astype(BF16)
-
-
-def backward(side, h, dy, wg, wu, wd, layer, wanted):
+        if gathered is not None:
+            others.finish()
+
+
+def backward(side, h, dy, wg, wu, wd, layer, wanted, shards=(), gathered=None):
     tokens, d = h.shape
     ff = wg.shape[2]
     tiles = ff // LANES
@@ -355,14 +529,18 @@
         *buffers(shapes2),
         pltpu.SemaphoreType.DMA((6, 2, 4)),
     ]
-    out_specs = [whole((rows, ff)), whole((rows, ff)), whole((down_rows, d)), whole((tokens, d))]
-    out_shape = [jax.ShapeDtypeStruct(s, BF16) for s in ((rows, ff), (rows, ff), (down_rows, d), (tokens, d))]
-    if wanted:
-        scratch.append(pltpu.VMEM((tokens, d), F32))
+    results = [(rows, ff), (rows, ff), (down_rows, d)] + [(tokens, d)] * wanted
+    out_specs = [whole(s) for s in results]
+    out_shape = [jax.ShapeDtypeStruct(s, BF16) for s in results]
+    scratch.append(pltpu.VMEM((tokens, d), F32 if wanted else BF16))
+    if shards:
+        out_specs += [pl.BlockSpec(memory_space=pl.ANY)] * 3
+        out_shape += [jax.ShapeDtypeStruct(w.shape, w.dtype) for w in (wg, wu, wd)]
+        scratch += gather_scratch(side)
     return pl.pallas_call(
-        functools.partial(backward_kernel, side, wanted),
+        functools.partial(backward_kernel, side, wanted, gathered),
         grid=(steps + 1,),
-        in_specs=[pl.BlockSpec(memory_space=pl.ANY), whole((tokens, d)), *across, *across, *down],
+        in_specs=[pl.BlockSpec(memory_space=pl.ANY), whole((tokens, d)), *across, *across, *down, *(whole(s.shape) for s in shards)],
         out_specs=out_specs,
         out_shape=out_shape,
         scratch_shapes=scratch,
@@ -371,121 +549,42 @@
         ),
         compiler_params=pltpu.CompilerParams(vmem_limit_bytes=63 * 2**20, collective_id=1 + layer, has_side_effects=True),
         name=f"backward_{layer}",
-    )(h, dy, *[wg] * side, *[wu] * side, *[wd] * side)
-
-
-def gather_kernel(side, *refs):
-    count = len(refs) // 2 - 1
-    shards, outs, (sems, local_sems) = refs[:count], refs[count : 2 * count], refs[2 * count :]
+    )(h, dy, *[wg] * side, *[wu] * side, *[wd] * side, *shards)
+
+
+def gather_kernel(side, layer, *refs):
+    shards, outs, (sems, local_sems) = refs[:3], refs[6:9], refs[9:]
     ring = Ring(side)
     ring.meet()
-    units = [(i, n) for n in reversed(range(shards[0].shape[0])) for i in range(count)]
-    me = ring.at[0] * side + ring.at[1]
-
-    def rows_of(i, first, many=1):
-        rows = shards[i].shape[1]
-        return pl.ds(pl.multiple_of(first * rows, 8), many * rows)
-
-    def halves(ref, i, n, first, many, half):
-        rows, columns = shards[i].shape[1:]
-        if columns % (2 * LANES) == 0:
-            return ref.at[n, rows_of(i, first, many), pl.ds(half * (columns // 2), columns // 2)]
-        length = many * rows // 2
-        return ref.at[n, pl.ds(pl.multiple_of(first * rows + half * length, 8), length)]
-
-    class Phase:
-        def __init__(self, number, i, n, axis, first, many, src):
-            self.number, self.i, self.n, self.axis, self.first, self.many, self.src = number, i, n, axis, first, many, src
-
-        def copy(self, src, dst, which, offset):
-            return pltpu.make_async_remote_copy(
-                src_ref=src,
-                dst_ref=dst,
-                send_sem=sems.at[0, self.number, which],
-                recv_sem=sems.at[1, self.number, which],
-                device_id=ring.device(self.axis, offset),
-                device_id_type=MESH,
-            )
-
-        def near(self, side):
-            dst = outs[self.i].at[self.n, rows_of(self.i, self.first(0), self.many)]
-            return self.copy(dst if self.src is None else self.src, dst, side, 1 - 2 * side)
-
-        def far(self, side):
-            offset = 1 - 2 * side
-            part = halves(outs[self.i], self.i, self.n, self.first(-offset), self.many, side)
-            return self.copy(part, part, 2 + side, offset)
-
-        def start(self):
-            for side in range(2):
-                self.near(side).start()
-
-        def relay(self):
-            for side in range(2):
-                self.near(side).wait_recv()
-                self.far(side).start()
-
-        def arrive(self):
-            for side in range(2):
-                self.far(side).wait_recv()
-
-        def finish(self):
-            for side in range(2):
-                self.near(side).wait_send()
-                self.far(side).wait_send()
-
-    one, two, number = {}, {}, 0
-    for i, n in units:
-        own = shards[i].at[n]
-        if n % 2:
-            one[i, n] = Phase(number, i, n, 1, lambda o: ring.at[0] * side + ring.place(1, o), 1, own)
-            two[i, n] = [Phase(number + 1, i, n, 0, lambda o: ring.place(0, o) * side, side, None)]
-        else:
-            one[i, n] = Phase(number, i, n, 0, lambda o: ring.place(0, o) * side + ring.at[1], 1, own)
-            two[i, n] = [
-                Phase(number + 1 + k, i, n, 1, lambda o, k=k: k * side + ring.place(1, o), 1, None) for k in range(side)
-            ]
-        number += 1 + len(two[i, n])
-
-    def local(i, n):
-        return pltpu.make_async_copy(shards[i].at[n], outs[i].at[n, rows_of(i, me)], local_sems.at[i, n])
-
-    for unit in units:
-        one[unit].start()
-        local(*unit).start()
-    for unit in units:
-        one[unit].relay()
-    for unit in units:
-        one[unit].arrive()
-        local(*unit).wait()
-        for phase in two[unit]:
-            phase.start()
-    for unit in units:
-        for phase in two[unit]:
-            phase.relay()
-    for unit in units:
-        for phase in two[unit]:
-            phase.arrive()
-    for unit in units:
-        for phase in (one[unit], *two[unit]):
-            phase.finish()
-
-
-def gather(side, shards):
-    layers = shards[0].shape[0]
-    phases = len(shards) * sum(2 if n % 2 else 1 + side for n in range(layers))
+    all_of = Gather(ring, shards, outs, layer, sems, local_sems)
+    all_of.start()
+    all_of.relay()
+    all_of.arrive()
+    for pair in all_of.pairs:
+        for piece in pair:
+            piece.start()
+    for pair in all_of.pairs:
+        for piece in pair:
+            piece.relay()
+    all_of.finish()
+
+
+def gather_scratch(side):
+    return [pltpu.SemaphoreType.DMA((2, 6 * (1 + side), 4)), pltpu.SemaphoreType.DMA((3,))]
+
+
+def gather(side, layer, shards, weights):
+    hbm = pl.BlockSpec(memory_space=pl.ANY)
     return pl.pallas_call(
-        functools.partial(gather_kernel, side),
-        in_specs=[pl.BlockSpec(memory_space=pltpu.VMEM)] * len(shards),
-        out_specs=[pl.BlockSpec(memory_space=pl.ANY)] * len(shards),
-        out_shape=[jax.ShapeDtypeStruct((layers, s.shape[1] * side**2, s.shape[2]), s.dtype) for s in shards],
-        scratch_shapes=[
-            pltpu.SemaphoreType.DMA((2, phases, 4)),
-            pltpu.SemaphoreType.DMA((len(shards), layers)),
-        ],
+        functools.partial(gather_kernel, side, layer),
+        in_specs=[pl.BlockSpec(memory_space=pltpu.VMEM)] * 3 + [hbm] * 3,
+        out_specs=[hbm] * 3,
+        out_shape=[jax.ShapeDtypeStruct(w.shape, w.dtype) for w in weights],
+        input_output_aliases={3: 0, 4: 1, 5: 2},
+        scratch_shapes=gather_scratch(side),
         compiler_params=pltpu.CompilerParams(vmem_limit_bytes=60 * 2**20, collective_id=0, has_side_effects=True),
         name="gather",
-    )(*shards)
+    )(*shards, *weights)
 
 
 def solution(mesh):
@@ -501,18 +600,25 @@
         for n in range(layers - 1):
             states.append(forward(states[-1], *weights, n))
 
-        grads = [None] * layers
+        def of_mine(which):
+            w, rows = weights[which], ms[which].shape[1]
+            return lax.dynamic_slice_in_dim(w, me * rows, rows, 1).astype(F32)
+
+        def fresh(n):
+            return [adamw(of_mine(i)[n], ms[i][n], vs[i][n], grads[n][i].astype(F32))[0] for i in range(3)]
+
+        grads, shards = [None] * layers, ()
         for n in reversed(range(layers)):
-            *grads[n], dy = backward(side, states[n], dy, *weights, n, n > 0)
-        new = []
-        for which in range(3):
-            w, m, v = weights[which], ms[which], vs[which]
-            rows = m.shape[1]
-            mine = lax.dynamic_slice_in_dim(w, me * rows, rows, 1)
-            g = jnp.stack([grads[n][which] for n in range(layers)])
-            new.append(adamw(mine.astype(F32), m, v, g.astype(F32)))
-        gathered = gather(side, [one[0] for one in new])
-        return (*gathered, *(one[1] for one in new), *(one[2] for one in new))
+            *out, = backward(side, states[n], dy, *weights, n, n > 0, shards, n + 1 if shards else None)
+            grads[n], gathered = out[:3], out[-3:]
+            dy = out[3]
+            shards = fresh(n)
+        gathered = gather(side, 0, shards, gathered)
+        moments = []
+        for i in range(3):
+            g = jnp.stack([grads[n][i] for n in range(layers)]).astype(F32)
+            moments.append(adamw(of_mine(i), ms[i], vs[i], g)[1:])
+        return (*gathered, *(one[0] for one in moments), *(one[1] for one in moments))
 
     tokens, row = P(("rep", "dp"), None, None), P(None, "dp", None)
     return jax.shard_map(

time: 694 us -> 652 us (0.939)
  Pallas kernels: 653 us -> 592 us
  other arithmetic: 9.54 us -> 30.8 us
    pallas_call x3, Pallas kernels: 598 us -> 537 us  [the longest x2 441 us: backward(): pl.pallas_call(functools.partial(backward_kernel, side, wanted, gathered)...]
    add x0 -> x3, other arithmetic: none -> 8.6 us  [adamw(): v = 0.95 * v + 0.05 * g * g]
    convert_element_type x0 -> x3, other arithmetic: none -> 7.29 us  [of_mine(): return lax.dynamic_slice_in_dim(w, me * rows, rows, 1).astype(F32)]
    convert_element_type x2 -> x5, other arithmetic: 9.54 us -> 14.9 us  [adamw(): return ((w - 0.02 * step).astype(BF16), m, v)]
    unnamed x31 -> x49, local copies, waits for them, and re-layouts: 27.5 us -> 24.2 us
where the time goes in v2:
time: 652 us; the launch traced here: 648 us
  Pallas kernels  592 us (91%)
  other arithmetic  30.8 us (5%)
  local copies, waits for them, and re-layouts  24.2 us (4%)
    pallas_call x2, Pallas kernels, backward(): pl.pallas_call(functools.partial(backward_kernel, side, wanted, gathered)...  441 us
    pallas_call x1, Pallas kernels, gather(): pl.pallas_call(functools.partial(gather_kernel, side, layer), in_specs=[p...  95.6 us
    pallas_call x1, Pallas kernels, forward(): pl.pallas_call(forward_kernel, grid=(ff // BLOCK,), in_specs=[whole((toke...  55 us
    unnamed x49, local copies, waits for them, and re-layouts  24.2 us
    convert_element_type x5, other arithmetic, adamw(): return ((w - 0.02 * step).astype(BF16), m, v)  14.9 us

profile of v2, /device:TPU:98, one launch (start us, length us, event | category | flops | bytes accessed | tf_op | source)
XLA Modules:
  0.0 647.9 jit_solution(6292698128290703376)
XLA Ops:
  0.6 2.4 dynamic-slice_convert_fusion
  3.1 2.4 dynamic-slice_convert_fusion.2
  5.5 2.4 dynamic-slice_convert_fusion.1
  7.9 55.0 %forward.1.h_hbm = bf16[2048,896]{1,0:T(8,128)(2,1)} custom-call(bf16[2048,896]{1,0:T(8,128)(2,1)} %bitcast.67, bf16[2,896,3584]{2,1,0:T(8,128)(2,1)} %refs_3_.3, bf16[2,896,3584]{2,1,0:T(8,128)(2,1)} %refs_7_.3, bf16[2,3584,896]{2,1,0:T(8,128)(2,1)} %refs_11_.3), custom_call_target="tpu_custom_call" | custom-call | flops 39460012032 | bytes 19267584 | tf_op jit(solution)/shard_map/forward/pallas_call | solution.py:72
  63.0 215.0 %backward_1.1 = (bf16[56,3584]{1,0:T(8,128)(2,1)}, bf16[56,3584]{1,0:T(8,128)(2,1)}, bf16[224,896]{1,0:T(8,128)(2,1)}, bf16[2048,896]{1,0:T(8,128)(2,1)}) custom-call(bf16[2048,896]{1,0:T(8,128)(2,1)} %forward.1.h_hbm, bf16[2048,896]{1,0:T(8,128)(2,1)} %bitcast.66, bf16[2,896,3584]{2,1,0:T(8,128)(2,1)} %refs_3_.3, bf16[2,896,3584]{2,1,0:T(8,128)(2,1)} %refs_3_.3, ...), custom_call_target="tpu_custom_call" | custom-call | flops 105226698752 | bytes 38535168 | tf_op jit(solution)/shard_map/backward_1/pallas_call | solution.py:540
  277.9 0.0 copy-start.1
  278.0 0.0 copy-start.3
  278.0 3.1 fusion.23.refs_14_
  281.0 0.0 copy-done.1
  281.0 3.8 fusion.11
  284.8 226.2 %backward_0.1 = (bf16[56,3584]{1,0:T(8,128)(2,1)}, bf16[56,3584]{1,0:T(8,128)(2,1)}, bf16[224,896]{1,0:T(8,128)(2,1)}, bf16[2,896,3584]{2,1,0:T(8,128)(2,1)}, bf...) custom-call(bf16[2048,896]{1,0:T(8,128)(2,1)} %bitcast.68, bf16[2048,896]{1,0:T(8,128)(2,1)} %get-tuple-element.22.dy_ref, ...), custom_call_target="tpu_custom_call" | custom-call | flops 78920024064 | bytes 38535168 | tf_op jit(solution)/shard_map/backward_0/pallas_call | solution.py:540
  511.1 0.0 copy-start.2
  511.1 0.0 copy-start.4
  511.1 3.1 fusion.41.refs_2_
  514.2 0.0 copy-done.4
  514.2 0.0 copy-start.7
  514.2 2.6 fusion.35.refs_1_
  516.8 2.4 fusion.29.refs_0_
  519.2 95.6 %gather.1 = (bf16[2,896,3584]{2,1,0:T(8,128)(2,1)}, bf16[2,896,3584]{2,1,0:T(8,128)(2,1)}, bf16[2,3584,896]{2,1,0:T(8,128)(2,1)}) custom-call(bf16[56,3584]{1,0:T(8,128)(2,1)} %fusion.29.refs_0_, bf16[56,3584]{1,0:T(8,128)(2,1)} %fusion.35.refs_1_, bf16[224,896]{1,0:T(8,128)(2,1)} %fusion.41.refs_2_, ...), custom_call_target="tpu_custom_call", output_to_operand_aliasing={{0}: (3, {}), {1}: (4, {}), {2}: (5, {})} | custom-call | tf_op jit(solution)/shard_map/gather/pallas_call | solution.py:578
  614.9 0.0 copy-start.6
  614.9 0.0 copy-start.8
  614.9 4.2 fusion.5
  619.1 2.2 fusion.4
  621.4 0.0 slice-start
  621.4 2.2 fusion.3
  623.6 2.6 copy-done
  626.1 0.0 slice-start.5
  626.1 6.5 %copy.29 = bf16[2,896,3584]{2,1,0:T(8,128)(2,1)} copy(bf16[2,896,3584]{2,1,0:T(8,128)(2,1)S(1)} %copy-done) | data formatting | bytes 25690112
  632.6 1.9 slice-done.2
  634.5 6.5 %copy.30 = bf16[2,896,3584]{2,1,0:T(8,128)(2,1)} copy(bf16[2,896,3584]{2,1,0:T(8,128)(2,1)S(1)} %bitcast.57) | data formatting | bytes 25690112
  641.0 1.8 slice-done.6
  642.8 4.9 copy.31
  (34 shorter events, 0.1 us)
Async XLA Ops:
  277.9 3.1 copy-start.1
  278.0 3.1 copy-start.3
  511.1 3.1 copy-start.2
  511.1 3.1 copy-start.4
  514.2 2.6 copy-start.5
  514.2 2.6 copy-start.7
  519.2 95.6 %copy-start.11 = (bf16[224,896]{1,0:T(8,128)(2,1)S(1)}, bf16[224,896]{1,0:T(8,128)(2,1)}, u32[]{:S(2)}) copy-start(bf16[224,896]{1,0:T(8,128)(2,1)} %get-tuple-element.25) | copy-start | bytes 1204228
  519.2 95.6 %copy-start.14 = (bf16[224,896]{1,0:T(8,128)(2,1)S(1)}, bf16[224,896]{1,0:T(8,128)(2,1)}, u32[]{:S(2)}) copy-start(bf16[224,896]{1,0:T(8,128)(2,1)} %get-tuple-element.28) | copy-start | bytes 1204228
  614.8 4.3 copy-start.10
  614.9 4.3 copy-start.13
  614.9 6.5 %copy-start.6 = (f32[2,56,3584]{2,1,0:T(8,128)S(1)}, f32[2,56,3584]{2,1,0:T(8,128)}, u32[]{:S(2)}) copy-start(f32[2,56,3584]{2,1,0:T(8,128)} %param.19) | copy-start | bytes 4816900
  614.9 6.5 %copy-start.8 = (f32[2,56,3584]{2,1,0:T(8,128)S(1)}, f32[2,56,3584]{2,1,0:T(8,128)}, u32[]{:S(2)}) copy-start(f32[2,56,3584]{2,1,0:T(8,128)} %param.16) | copy-start | bytes 4816900
  614.9 6.5 copy-start.9
  614.9 6.5 copy-start.12
  619.1 7.0 %copy-start = (bf16[2,896,3584]{2,1,0:T(8,128)(2,1)S(1)}, bf16[2,896,3584]{2,1,0:T(8,128)(2,1)}, u32[]{:S(2)}) copy-start(bf16[2,896,3584]{2,1,0:T(8,128)(2,1)} %get-tuple-element.52) | copy-start | bytes 38535172
  621.4 11.3 %slice-start = ((s8[12845056]{0:T(1024)(128)(4,1)}), s8[4194304]{0:T(1024)(128)(4,1)S(1)}, s32[]{:S(2)}) async-start(s8[12845056]{0:T(1024)(128)(4,1)} %bitcast.56), calls=%async_computation | async-start | bytes 8388608
  626.1 6.5 %slice-start.1 = ((s8[12845056]{0:T(1024)(128)(4,1)}), s8[4194304]{0:T(1024)(128)(4,1)S(1)}, s32[]{:S(2)}) async-start(s8[12845056]{0:T(1024)(128)(4,1)} %bitcast.56), calls=%async_computation.1 | async-start | bytes 8388608
  626.1 8.4 %slice-start.2 = ((s8[12845056]{0:T(1024)(128)(4,1)}), s8[4194304]{0:T(1024)(128)(4,1)S(1)}, s32[]{:S(2)}) async-start(s8[12845056]{0:T(1024)(128)(4,1)} %bitcast.56), calls=%async_computation.2 | async-start | bytes 8388608
  626.1 8.4 %slice-start.3 = ((s8[12845056]{0:T(1024)(128)(4,1)}), s8[262144]{0:T(1024)(128)(4,1)S(1)}, s32[]{:S(2)}) async-start(s8[12845056]{0:T(1024)(128)(4,1)} %bitcast.56), calls=%async_computation.3 | async-start | bytes 524288
  626.1 14.9 %slice-start.4 = ((s8[12845056]{0:T(1024)(128)(4,1)}), s8[4194304]{0:T(1024)(128)(4,1)S(1)}, s32[]{:S(2)}) async-start(s8[12845056]{0:T(1024)(128)(4,1)} %bitcast.58), calls=%async_computation.4 | async-start | bytes 8388608
  626.1 14.9 %slice-start.5 = ((s8[12845056]{0:T(1024)(128)(4,1)}), s8[4194304]{0:T(1024)(128)(4,1)S(1)}, s32[]{:S(2)}) async-start(s8[12845056]{0:T(1024)(128)(4,1)} %bitcast.58), calls=%async_computation.5 | async-start | bytes 8388608
  634.5 8.3 %slice-start.6 = ((s8[12845056]{0:T(1024)(128)(4,1)}), s8[4194304]{0:T(1024)(128)(4,1)S(1)}, s32[]{:S(2)}) async-start(s8[12845056]{0:T(1024)(128)(4,1)} %bitcast.58), calls=%async_computation.6 | async-start | bytes 8388608
  634.5 8.3 %slice-start.7 = ((s8[12845056]{0:T(1024)(128)(4,1)}), s8[262144]{0:T(1024)(128)(4,1)S(1)}, s32[]{:S(2)}) async-start(s8[12845056]{0:T(1024)(128)(4,1)} %bitcast.58), calls=%async_computation.7 | async-start | bytes 524288

commit v3 on v2

--- a/solution.py
+++ b/solution.py
@@ -25,11 +25,14 @@
     return (wide * scale).astype(BF16)
 
 
+def moments(m, v, g):
+    return 0.9 * m + 0.1 * g, 0.95 * v + 0.05 * g * g
+
+
 def adamw(w, m, v, g):
-    m = 0.9 * m + 0.1 * g
-    v = 0.95 * v + 0.05 * g * g
+    m, v = moments(m, v, g)
     step = m * lax.rsqrt(v + 1e-8) + 0.1 * w
-    return (w - 0.02 * step).astype(BF16), m, v
+    return (w - 0.02 * step).astype(BF16)
 
 
 def whole(shape):
@@ -360,12 +363,37 @@
             mine = [g[rows * (side * x + place) : rows * (side * x + place + 1), LANES:] for x in range(side)]
             gb[place, half] = jnp.concatenate(mine, 0).astype(BF16)
 
-    computing, summing = t < steps, t > 0
+    def own(total):
+        return lambda place, half: total[half, pl.ds(pl.multiple_of(place * rows, 8), rows)]
+
+    def mine(place, half):
+        return sd[pl.ds(pl.multiple_of((2 * place + half) * half_d, 8), half_d)]
+
+    def second_relay():
+        second_a.relay(own(sa))
+        second_b.relay(own(sb))
+
+    def second_end(run):
+        second_a.arrive()
+        second_b.arrive()
+        for two, total, tile in ((second_a, sa, 0), (second_b, sb, 1)):
+            place = ring.place(two.axis, 0)
+            for half, out in enumerate((gg_ref, gu_ref)):
+                value = (own(total)(place, half) + two.received(half)).astype(BF16)
+                for j in range(value.shape[1] // LANES):
+                    lane = pl.multiple_of((run + steps * (tile + j)) * LANES, LANES)
+                    out[:, pl.ds(lane, LANES)] = value[:, j * LANES : (j + 1) * LANES]
+
+    computing, summing, ending = t < steps, t > 0, t > 1
 
     @pl.when(computing)
     def _():
         chunk(0)
         chunk(1)
+
+    @pl.when(ending)
+    def _():
+        second_relay()
 
     @pl.when(summing)
     def _():
@@ -392,6 +420,10 @@
         @pl.when(t == 0)
         def _():
             others.relay()
+
+    @pl.when(ending)
+    def _():
+        second_end(t - 2)
 
     @pl.when(summing)
     def _():
@@ -411,9 +443,6 @@
             count = value.shape[0]
             sd[pl.ds(pl.multiple_of((2 * (t - 1) + half) * count, count), count)] = value
 
-    def mine(place, half):
-        return sd[pl.ds(pl.multiple_of((2 * place + half) * half_d, 8), half_d)]
-
     @pl.when(t == steps)
     def _():
         for p in range(side):
@@ -427,43 +456,22 @@
         gd[...] = held_ref[...]
         for half in range(2):
             first_d.first(half).start()
+
+    beside(True)
+
+    @pl.when(computing)
+    def _():
         g = dot(at_ref[...], dgate_ref[...])
         put(g, 0)
         first_a.first(0).start()
         first_b.first(0).start()
 
-    def own(total):
-        return lambda place, half: total[half, pl.ds(pl.multiple_of(place * rows, 8), rows)]
-
-    @pl.when(summing)
-    def _():
-        second_a.relay(own(sa))
-        second_b.relay(own(sb))
-
-    @pl.when(t == steps)
-    def _():
-        second_d.relay(mine)
-
-    beside(True)
-
     @pl.when(computing)
     def _():
         g = dot(at_ref[...], dup_ref[...])
         put(g, 1)
         first_a.first(1).start()
         first_b.first(1).start()
-
-    @pl.when(summing)
-    def _():
-        second_a.arrive()
-        second_b.arrive()
-        for two, total, tile in ((second_a, sa, 0), (second_b, sb, 1)):
-            place = ring.place(two.axis, 0)
-            for half, out in enumerate((gg_ref, gu_ref)):
-                value = (own(total)(place, half) + two.received(half)).astype(BF16)
-                for j in range(value.shape[1] // LANES):
-                    lane = pl.multiple_of((t - 1 + steps * (tile + j)) * LANES, LANES)
-                    out[:, pl.ds(lane, LANES)] = value[:, j * LANES : (j + 1) * LANES]
 
     if wanted:
 
@@ -480,6 +488,9 @@
 
     @pl.when(t == steps)
     def _():
+        second_relay()
+        second_d.relay(mine)
+        second_end(t - 1)
         second_d.arrive()
         place = ring.place(1, 0)
         for half in range(2):
@@ -600,12 +611,13 @@
         for n in range(layers - 1):
             states.append(forward(states[-1], *weights, n))
 
-        def of_mine(which):
-            w, rows = weights[which], ms[which].shape[1]
-            return lax.dynamic_slice_in_dim(w, me * rows, rows, 1).astype(F32)
-
         def fresh(n):
-            return [adamw(of_mine(i)[n], ms[i][n], vs[i][n], grads[n][i].astype(F32))[0] for i in range(3)]
+            new = []
+            for i in range(3):
+                rows, columns = ms[i].shape[1:]
+                w = lax.dynamic_slice(weights[i], (n, me * rows, 0), (1, rows, columns))[0]
+                new.append(adamw(w.astype(F32), ms[i][n], vs[i][n], grads[n][i].astype(F32)))
+            return new
 
         grads, shards = [None] * layers, ()
         for n in reversed(range(layers)):
@@ -614,11 +626,11 @@
             dy = out[3]
             shards = fresh(n)
         gathered = gather(side, 0, shards, gathered)
-        moments = []
+        after = []
         for i in range(3):
             g = jnp.stack([grads[n][i] for n in range(layers)]).astype(F32)
-            moments.append(adamw(of_mine(i), ms[i], vs[i], g)[1:])
-        return (*gathered, *(one[0] for one in moments), *(one[1] for one in moments))
+            after.append(moments(ms[i], vs[i], g))
+        return (*gathered, *(one[0] for one in after), *(one[1] for one in after))
 
     tokens, row = P(("rep", "dp"), None, None), P(None, "dp", None)
     return jax.shard_map(

time: 652 us -> 622 us (0.954)
  Pallas kernels: 592 us -> 571 us
  other arithmetic: 30.8 us -> 23.1 us
    pallas_call x2, Pallas kernels: 441 us -> 420 us  [backward(): pl.pallas_call(functools.partial(backward_kernel, side, wanted, gathered)...]
    convert_element_type x8 -> x5, other arithmetic: 22.2 us -> 14.3 us  [adamw(): return (w - 0.02 * step).astype(BF16)]
where the time goes in v3:
time: 622 us; the launch traced here: 618 us
  Pallas kernels  571 us (92%)
  local copies, waits for them, and re-layouts  23.2 us (4%)
  other arithmetic  23.1 us (4%)
    pallas_call x2, Pallas kernels, backward(): pl.pallas_call(functools.partial(backward_kernel, side, wanted, gathered)...  420 us
    pallas_call x1, Pallas kernels, gather(): pl.pallas_call(functools.partial(gather_kernel, side, layer), in_specs=[p...  95.5 us
    pallas_call x1, Pallas kernels, forward(): pl.pallas_call(forward_kernel, grid=(ff // BLOCK,), in_specs=[whole((toke...  55.1 us
    unnamed x49, local copies, waits for them, and re-layouts  23.2 us
    convert_element_type x5, other arithmetic, adamw(): return (w - 0.02 * step).astype(BF16)  14.3 us

profile of v3, /device:TPU:98, one launch (start us, length us, event | category | flops | bytes accessed | tf_op | source)
XLA Modules:
  0.0 618.4 jit_solution(11115505312194857414)
XLA Ops:
  0.6 55.1 %forward.1.h_hbm = bf16[2048,896]{1,0:T(8,128)(2,1)} custom-call(bf16[2048,896]{1,0:T(8,128)(2,1)} %bitcast.61, bf16[2,896,3584]{2,1,0:T(8,128)(2,1)} %refs_3_.3, bf16[2,896,3584]{2,1,0:T(8,128)(2,1)} %refs_7_.3, bf16[2,3584,896]{2,1,0:T(8,128)(2,1)} %refs_11_.3), custom_call_target="tpu_custom_call" | custom-call | flops 39460012032 | bytes 19267584 | tf_op jit(solution)/shard_map/forward/pallas_call | solution.py:75
  55.7 202.6 %backward_1.1 = (bf16[56,3584]{1,0:T(8,128)(2,1)}, bf16[56,3584]{1,0:T(8,128)(2,1)}, bf16[224,896]{1,0:T(8,128)(2,1)}, bf16[2048,896]{1,0:T(8,128)(2,1)}) custom-call(bf16[2048,896]{1,0:T(8,128)(2,1)} %forward.1.h_hbm, bf16[2048,896]{1,0:T(8,128)(2,1)} %bitcast.60, bf16[2,896,3584]{2,1,0:T(8,128)(2,1)} %refs_3_.3, bf16[2,896,3584]{2,1,0:T(8,128)(2,1)} %refs_3_.3, ...), custom_call_target="tpu_custom_call" | custom-call | flops 105226698752 | bytes 38535168 | tf_op jit(solution)/shard_map/backward_1/pallas_call | solution.py:551
  258.3 0.0 copy-start.3
  258.4 0.0 copy-start.10
  258.4 0.0 copy-start.11
  258.4 2.9 fusion.32.refs_14_
  261.3 0.0 copy-done.10
  261.3 3.6 fusion.30
  265.0 217.8 %backward_0.1 = (bf16[56,3584]{1,0:T(8,128)(2,1)}, bf16[56,3584]{1,0:T(8,128)(2,1)}, bf16[224,896]{1,0:T(8,128)(2,1)}, bf16[2,896,3584]{2,1,0:T(8,128)(2,1)}, bf...) custom-call(bf16[2048,896]{1,0:T(8,128)(2,1)} %bitcast.62, bf16[2048,896]{1,0:T(8,128)(2,1)} %get-tuple-element.22.dy_ref, ...), custom_call_target="tpu_custom_call" | custom-call | flops 78920024064 | bytes 38535168 | tf_op jit(solution)/shard_map/backward_0/pallas_call | solution.py:551
  482.8 0.0 copy-start.6
  482.8 0.0 copy-start.5
  482.8 2.9 fusion.35.refs_2_
  485.8 2.6 fusion.33.refs_0_
  488.3 0.0 copy-done.4
  488.4 2.2 fusion.34.refs_1_
  490.6 95.5 %gather.1 = (bf16[2,896,3584]{2,1,0:T(8,128)(2,1)}, bf16[2,896,3584]{2,1,0:T(8,128)(2,1)}, bf16[2,3584,896]{2,1,0:T(8,128)(2,1)}) custom-call(bf16[56,3584]{1,0:T(8,128)(2,1)} %fusion.33.refs_0_, bf16[56,3584]{1,0:T(8,128)(2,1)} %fusion.34.refs_1_, bf16[224,896]{1,0:T(8,128)(2,1)} %fusion.35.refs_2_, ...), custom_call_target="tpu_custom_call", output_to_operand_aliasing={{0}: (3, {}), {1}: (4, {}), {2}: (5, {})} | custom-call | tf_op jit(solution)/shard_map/gather/pallas_call | solution.py:589
  586.0 0.0 copy-start.7
  586.0 0.0 copy-start.8
  586.1 0.0 copy-start.1
  586.1 0.0 copy-start.2
  586.1 0.0 copy-start.9
  586.1 3.3 fusion.4
  589.4 3.3 fusion.3
  592.8 0.0 slice-start
  592.8 2.2 fusion.5
  595.0 1.7 copy-done
  596.7 0.0 slice-start.5
  596.7 6.5 %copy.29 = bf16[2,896,3584]{2,1,0:T(8,128)(2,1)} copy(bf16[2,896,3584]{2,1,0:T(8,128)(2,1)S(1)} %copy-done) | data formatting | bytes 25690112
  603.2 1.7 slice-done.2
  605.0 6.5 %copy.30 = bf16[2,896,3584]{2,1,0:T(8,128)(2,1)} copy(bf16[2,896,3584]{2,1,0:T(8,128)(2,1)S(1)} %bitcast.51) | data formatting | bytes 25690112
  611.5 1.8 slice-done.6
  613.3 4.9 copy.31
  (31 shorter events, 0.1 us)
Async XLA Ops:
  258.3 3.0 copy-start.3
  258.4 3.0 copy-start.10
  258.4 3.0 copy-start.11
  482.8 3.0 copy-start.6
  482.8 3.0 copy-start.13
  482.8 5.6 copy-start.5
  485.8 2.6 copy-start.4
  485.8 2.6 copy-start.14
  586.0 3.4 copy-start.7
  586.0 3.4 copy-start.8
  586.1 6.7 %copy-start.1 = (f32[2,224,896]{2,1,0:T(8,128)S(1)}, f32[2,224,896]{2,1,0:T(8,128)}, u32[]{:S(2)}) copy-start(f32[2,224,896]{2,1,0:T(8,128)} %param.21) | copy-start | bytes 4816900
  586.1 6.7 %copy-start.2 = (f32[2,224,896]{2,1,0:T(8,128)S(1)}, f32[2,224,896]{2,1,0:T(8,128)}, u32[]{:S(2)}) copy-start(f32[2,224,896]{2,1,0:T(8,128)} %param.18) | copy-start | bytes 4816900
  586.1 6.7 %copy-start.9 = (bf16[224,896]{1,0:T(8,128)(2,1)S(1)}, bf16[224,896]{1,0:T(8,128)(2,1)}, u32[]{:S(2)}) copy-start(bf16[224,896]{1,0:T(8,128)(2,1)} %get-tuple-element.25) | copy-start | bytes 1204228
  586.1 6.7 %copy-start.12 = (bf16[224,896]{1,0:T(8,128)(2,1)S(1)}, bf16[224,896]{1,0:T(8,128)(2,1)}, u32[]{:S(2)}) copy-start(bf16[224,896]{1,0:T(8,128)(2,1)} %get-tuple-element.28) | copy-start | bytes 1204228
  589.4 7.3 %copy-start = (bf16[2,896,3584]{2,1,0:T(8,128)(2,1)S(1)}, bf16[2,896,3584]{2,1,0:T(8,128)(2,1)}, u32[]{:S(2)}) copy-start(bf16[2,896,3584]{2,1,0:T(8,128)(2,1)} %get-tuple-element.52) | copy-start | bytes 38535172
  592.8 10.4 %slice-start = ((s8[12845056]{0:T(1024)(128)(4,1)}), s8[4194304]{0:T(1024)(128)(4,1)S(1)}, s32[]{:S(2)}) async-start(s8[12845056]{0:T(1024)(128)(4,1)} %bitcast.50), calls=%async_computation | async-start | bytes 8388608
  596.7 6.5 %slice-start.1 = ((s8[12845056]{0:T(1024)(128)(4,1)}), s8[4194304]{0:T(1024)(128)(4,1)S(1)}, s32[]{:S(2)}) async-start(s8[12845056]{0:T(1024)(128)(4,1)} %bitcast.50), calls=%async_computation.1 | async-start | bytes 8388608
  596.7 8.3 %slice-start.2 = ((s8[12845056]{0:T(1024)(128)(4,1)}), s8[4194304]{0:T(1024)(128)(4,1)S(1)}, s32[]{:S(2)}) async-start(s8[12845056]{0:T(1024)(128)(4,1)} %bitcast.50), calls=%async_computation.2 | async-start | bytes 8388608
  596.7 8.3 %slice-start.3 = ((s8[12845056]{0:T(1024)(128)(4,1)}), s8[262144]{0:T(1024)(128)(4,1)S(1)}, s32[]{:S(2)}) async-start(s8[12845056]{0:T(1024)(128)(4,1)} %bitcast.50), calls=%async_computation.3 | async-start | bytes 524288
  596.7 14.8 %slice-start.4 = ((s8[12845056]{0:T(1024)(128)(4,1)}), s8[4194304]{0:T(1024)(128)(4,1)S(1)}, s32[]{:S(2)}) async-start(s8[12845056]{0:T(1024)(128)(4,1)} %bitcast.52), calls=%async_computation.4 | async-start | bytes 8388608
  596.7 14.8 %slice-start.5 = ((s8[12845056]{0:T(1024)(128)(4,1)}), s8[4194304]{0:T(1024)(128)(4,1)S(1)}, s32[]{:S(2)}) async-start(s8[12845056]{0:T(1024)(128)(4,1)} %bitcast.52), calls=%async_computation.5 | async-start | bytes 8388608
  605.0 8.3 %slice-start.6 = ((s8[12845056]{0:T(1024)(128)(4,1)}), s8[4194304]{0:T(1024)(128)(4,1)S(1)}, s32[]{:S(2)}) async-start(s8[12845056]{0:T(1024)(128)(4,1)} %bitcast.52), calls=%async_computation.6 | async-start | bytes 8388608
  605.0 8.3 %slice-start.7 = ((s8[12845056]{0:T(1024)(128)(4,1)}), s8[262144]{0:T(1024)(128)(4,1)S(1)}, s32[]{:S(2)}) async-start(s8[12845056]{0:T(1024)(128)(4,1)} %bitcast.52), calls=%async_computation.7 | async-start | bytes 524288

commit v4 on v3

--- a/solution.py
+++ b/solution.py
@@ -8,7 +8,7 @@
 from jax.experimental.pallas import tpu as pltpu
 from jax.sharding import PartitionSpec as P
 
-BLOCK = 256
+BLOCK = 512
 CHUNKS = 4
 LANES = 128
 MESH = pl.DeviceIdType.MESH
@@ -53,12 +53,14 @@
             acc_ref[rows] = jnp.zeros((CHUNK, x_ref.shape[1]), F32)
 
     wg, wu, wd = wg_ref[0], wu_ref[0], wd_ref[0]
-    for c in range(chunks):
-        rows = pl.ds(c * CHUNK, CHUNK)
-        a = a_ref[rows]
-        gate, up = dot(a, wg), dot(a, wu)
-        hidden = (gate * jax.nn.sigmoid(gate) * up).astype(BF16)
-        acc_ref[rows] += dot(hidden, wd)
+    @pl.loop(0, chunks // 2)
+    def _(i):
+        for c in range(2):
+            rows = pl.ds((2 * i + c) * CHUNK, CHUNK)
+            a = a_ref[rows]
+            gate, up = dot(a, wg), dot(a, wu)
+            hidden = (gate * jax.nn.sigmoid(gate) * up).astype(BF16)
+            acc_ref[rows] += dot(hidden, wd)
 
     @pl.when(f == pl.num_programs(0) - 1)
     def _():
@@ -329,8 +331,9 @@
         copy = pltpu.make_async_copy(h_hbm, h_ref, local_sem)
         copy.start()
         copy.wait()
-        for c in range(CHUNKS):
-            part = pl.ds(c * size, size)
+        @pl.loop(0, CHUNKS)
+        def _(c):
+            part = pl.ds(pl.multiple_of(c * size, size), size)
             a = normed(h_ref[part])
             a_ref[part] = a
             at_ref[:, part] = a.T
@@ -343,7 +346,7 @@
 
     def chunk(c):
         wg, wu, wd = joined(wg_refs, 1), joined(wu_refs, 1), joined(wd_refs, 0)
-        part = pl.ds(c * size, size)
+        part = pl.ds(pl.multiple_of(c * size, size), size)
         a = a_ref[part]
         gate, up = dot(a, wg), dot(a, wu)
         dhid = dot(dy_ref[part], wd, ((1,), (1,))).astype(BF16).astype(F32)
@@ -351,11 +354,12 @@
         silu = gate * s
         hid_ref[part] = (silu * up).astype(BF16)
         dup = (dhid * silu).astype(BF16)
-        dgate = (dhid * up * (s * (1 + gate * (1 - s)))).astype(BF16)
+        dgate = (dhid * up * (s + silu * (1 - s))).astype(BF16)
         dup_ref[part] = dup
         dgate_ref[part] = dgate
         if wanted:
-            da_ref[part] += dot(dgate, wg, ((1,), (1,))) + dot(dup, wu, ((1,), (1,)))
+            by_both = jnp.concatenate([dgate, dup], 1)
+            da_ref[part] += dot(by_both, jnp.concatenate([wg, wu], 1), ((1,), (1,)))
 
     def put(g, half):
         for place in range(side):
@@ -386,32 +390,37 @@
 
     computing, summing, ending = t < steps, t > 0, t > 1
 
+    def stages():
+        @pl.when(ending)
+        def _():
+            second_relay()
+
+        @pl.when(summing)
+        def _():
+            for one in (first_a, first_b, first_d):
+                one.relay()
+
+        if gathered is not None:
+
+            @pl.when(t == 1)
+            def _():
+                others.arrive()
+
+        beside(False)
+
+    @pl.loop(0, CHUNKS // 2)
+    def _(i):
+        @pl.when(computing)
+        def _():
+            chunk(2 * i)
+            chunk(2 * i + 1)
+
+        @pl.when(i == 0)
+        def _():
+            stages()
+
     @pl.when(computing)
     def _():
-        chunk(0)
-        chunk(1)
-
-    @pl.when(ending)
-    def _():
-        second_relay()
-
-    @pl.when(summing)
-    def _():
-        for one in (first_a, first_b, first_d):
-            one.relay()
-
-    if gathered is not None:
-
-        @pl.when(t == 1)
-        def _():
-            others.arrive()
-
-    beside(False)
-
-    @pl.when(computing)
-    def _():
-        chunk(2)
-        chunk(3)
         g = dot(dyt_ref[...], hid_ref[...]).T.astype(BF16)
         held_ref[...] = g.reshape(held_ref.shape)
 
@@ -477,8 +486,9 @@
 
         @pl.when(t == steps - 1)
         def _():
-            for c in range(CHUNKS):
-                part = pl.ds(c * size, size)
+            @pl.loop(0, CHUNKS)
+            def _(c):
+                part = pl.ds(pl.multiple_of(c * size, size), size)
                 wide = h_ref[part].astype(F32)
                 by_a = da_ref[part].astype(BF16).astype(F32)
                 scale = lax.rsqrt(jnp.mean(wide**2, -1, keepdims=True) + 1e-6)

time: 622 us -> 610 us (0.981)
  Pallas kernels: 571 us -> 562 us
    pallas_call x2, Pallas kernels: 420 us -> 408 us  [backward(): pl.pallas_call(functools.partial(backward_kernel, side, wanted, gathered)...]
where the time goes in v4:
time: 610 us; the launch traced here: 609 us
  Pallas kernels  562 us (92%)
  local copies, waits for them, and re-layouts  23.2 us (4%)
  other arithmetic  23.1 us (4%)
    pallas_call x2, Pallas kernels, backward(): pl.pallas_call(functools.partial(backward_kernel, side, wanted, gathered)...  408 us
    pallas_call x1, Pallas kernels, gather(): pl.pallas_call(functools.partial(gather_kernel, side, layer), in_specs=[p...  97 us
    pallas_call x1, Pallas kernels, forward(): pl.pallas_call(forward_kernel, grid=(ff // BLOCK,), in_specs=[whole((toke...  57 us
    unnamed x49, local copies, waits for them, and re-layouts  23.2 us
    convert_element_type x5, other arithmetic, adamw(): return (w - 0.02 * step).astype(BF16)  14.3 us

profile of v4, /device:TPU:98, one launch (start us, length us, event | category | flops | bytes accessed | tf_op | source)
XLA Modules:
  0.0 609.0 jit_solution(14564673104202026409)
XLA Ops:
  0.6 57.0 %forward.1.h_hbm = bf16[2048,896]{1,0:T(8,128)(2,1)} custom-call(bf16[2048,896]{1,0:T(8,128)(2,1)} %bitcast.61, bf16[2,896,3584]{2,1,0:T(8,128)(2,1)} %refs_3_.3, bf16[2,896,3584]{2,1,0:T(8,128)(2,1)} %refs_7_.3, bf16[2,3584,896]{2,1,0:T(8,128)(2,1)} %refs_11_.3), custom_call_target="tpu_custom_call" | custom-call | flops 39460012032 | bytes 19267584 | tf_op jit(solution)/shard_map/forward/pallas_call | solution.py:77
  57.6 191.8 %backward_1.1 = (bf16[56,3584]{1,0:T(8,128)(2,1)}, bf16[56,3584]{1,0:T(8,128)(2,1)}, bf16[224,896]{1,0:T(8,128)(2,1)}, bf16[2048,896]{1,0:T(8,128)(2,1)}) custom-call(bf16[2048,896]{1,0:T(8,128)(2,1)} %forward.1.h_hbm, bf16[2048,896]{1,0:T(8,128)(2,1)} %bitcast.60, bf16[2,896,3584]{2,1,0:T(8,128)(2,1)} %refs_3_.3, bf16[2,896,3584]{2,1,0:T(8,128)(2,1)} %refs_3_.3, ...), custom_call_target="tpu_custom_call" | custom-call | flops 105226698752 | bytes 38535168 | tf_op jit(solution)/shard_map/backward_1/pallas_call | solution.py:561
  249.4 0.0 copy-start.3
  249.4 2.9 fusion.32.refs_14_
  252.4 3.6 fusion.30
  256.0 216.0 %backward_0.1 = (bf16[56,3584]{1,0:T(8,128)(2,1)}, bf16[56,3584]{1,0:T(8,128)(2,1)}, bf16[224,896]{1,0:T(8,128)(2,1)}, bf16[2,896,3584]{2,1,0:T(8,128)(2,1)}, bf...) custom-call(bf16[2048,896]{1,0:T(8,128)(2,1)} %bitcast.62, bf16[2048,896]{1,0:T(8,128)(2,1)} %get-tuple-element.22.dy_ref, ...), custom_call_target="tpu_custom_call" | custom-call | flops 78920024064 | bytes 38535168 | tf_op jit(solution)/shard_map/backward_0/pallas_call | solution.py:561
  472.0 0.0 copy-start.6
  472.0 0.0 copy-start.13
  472.1 0.0 copy-start.5
  472.1 2.9 fusion.35.refs_2_
  475.0 2.6 fusion.33.refs_0_
  477.6 0.0 copy-done.5
  477.6 0.0 copy-done.14
  477.6 2.2 fusion.34.refs_1_
  479.8 97.0 %gather.1 = (bf16[2,896,3584]{2,1,0:T(8,128)(2,1)}, bf16[2,896,3584]{2,1,0:T(8,128)(2,1)}, bf16[2,3584,896]{2,1,0:T(8,128)(2,1)}) custom-call(bf16[56,3584]{1,0:T(8,128)(2,1)} %fusion.33.refs_0_, bf16[56,3584]{1,0:T(8,128)(2,1)} %fusion.34.refs_1_, bf16[224,896]{1,0:T(8,128)(2,1)} %fusion.35.refs_2_, ...), custom_call_target="tpu_custom_call", output_to_operand_aliasing={{0}: (3, {}), {1}: (4, {}), {2}: (5, {})} | custom-call | tf_op jit(solution)/shard_map/gather/pallas_call | solution.py:599
  576.9 0.0 copy-start.7
  576.9 0.0 copy-start.8
  576.9 0.0 copy-start.1
  576.9 0.0 copy-start.2
  576.9 0.0 copy-start.9
  576.9 0.0 copy-start.12
  576.9 3.3 fusion.4
  580.3 3.3 fusion.3
  583.6 0.0 slice-start
  583.6 2.2 fusion.5
  585.8 1.7 copy-done
  587.5 0.0 slice-start.5
  587.5 6.5 %copy.29 = bf16[2,896,3584]{2,1,0:T(8,128)(2,1)} copy(bf16[2,896,3584]{2,1,0:T(8,128)(2,1)S(1)} %copy-done) | data formatting | bytes 25690112
  594.1 1.7 slice-done.2
  595.8 6.5 %copy.30 = bf16[2,896,3584]{2,1,0:T(8,128)(2,1)} copy(bf16[2,896,3584]{2,1,0:T(8,128)(2,1)S(1)} %bitcast.51) | data formatting | bytes 25690112
  602.3 1.8 slice-done.6
  604.1 4.9 copy.31
  (31 shorter events, 0.1 us)
Async XLA Ops:
  249.4 3.0 copy-start.3
  249.4 3.0 copy-start.10
  249.4 3.0 copy-start.11
  472.0 3.0 copy-start.6
  472.0 3.0 copy-start.13
  472.1 5.6 copy-start.5
  475.0 2.6 copy-start.4
  475.0 2.6 copy-start.14
  576.9 3.4 copy-start.7
  576.9 3.4 copy-start.8
  576.9 6.7 %copy-start.1 = (f32[2,224,896]{2,1,0:T(8,128)S(1)}, f32[2,224,896]{2,1,0:T(8,128)}, u32[]{:S(2)}) copy-start(f32[2,224,896]{2,1,0:T(8,128)} %param.21) | copy-start | bytes 4816900
  576.9 6.7 %copy-start.2 = (f32[2,224,896]{2,1,0:T(8,128)S(1)}, f32[2,224,896]{2,1,0:T(8,128)}, u32[]{:S(2)}) copy-start(f32[2,224,896]{2,1,0:T(8,128)} %param.18) | copy-start | bytes 4816900
  576.9 6.7 %copy-start.9 = (bf16[224,896]{1,0:T(8,128)(2,1)S(1)}, bf16[224,896]{1,0:T(8,128)(2,1)}, u32[]{:S(2)}) copy-start(bf16[224,896]{1,0:T(8,128)(2,1)} %get-tuple-element.25) | copy-start | bytes 1204228
  576.9 6.7 %copy-start.12 = (bf16[224,896]{1,0:T(8,128)(2,1)S(1)}, bf16[224,896]{1,0:T(8,128)(2,1)}, u32[]{:S(2)}) copy-start(bf16[224,896]{1,0:T(8,128)(2,1)} %get-tuple-element.28) | copy-start | bytes 1204228
  580.3 7.3 %copy-start = (bf16[2,896,3584]{2,1,0:T(8,128)(2,1)S(1)}, bf16[2,896,3584]{2,1,0:T(8,128)(2,1)}, u32[]{:S(2)}) copy-start(bf16[2,896,3584]{2,1,0:T(8,128)(2,1)} %get-tuple-element.52) | copy-start | bytes 38535172
  583.6 10.4 %slice-start = ((s8[12845056]{0:T(1024)(128)(4,1)}), s8[4194304]{0:T(1024)(128)(4,1)S(1)}, s32[]{:S(2)}) async-start(s8[12845056]{0:T(1024)(128)(4,1)} %bitcast.50), calls=%async_computation | async-start | bytes 8388608
  587.5 6.5 %slice-start.1 = ((s8[12845056]{0:T(1024)(128)(4,1)}), s8[4194304]{0:T(1024)(128)(4,1)S(1)}, s32[]{:S(2)}) async-start(s8[12845056]{0:T(1024)(128)(4,1)} %bitcast.50), calls=%async_computation.1 | async-start | bytes 8388608
  587.5 8.3 %slice-start.2 = ((s8[12845056]{0:T(1024)(128)(4,1)}), s8[4194304]{0:T(1024)(128)(4,1)S(1)}, s32[]{:S(2)}) async-start(s8[12845056]{0:T(1024)(128)(4,1)} %bitcast.50), calls=%async_computation.2 | async-start | bytes 8388608
  587.5 8.3 %slice-start.3 = ((s8[12845056]{0:T(1024)(128)(4,1)}), s8[262144]{0:T(1024)(128)(4,1)S(1)}, s32[]{:S(2)}) async-start(s8[12845056]{0:T(1024)(128)(4,1)} %bitcast.50), calls=%async_computation.3 | async-start | bytes 524288
  587.5 14.8 %slice-start.4 = ((s8[12845056]{0:T(1024)(128)(4,1)}), s8[4194304]{0:T(1024)(128)(4,1)S(1)}, s32[]{:S(2)}) async-start(s8[12845056]{0:T(1024)(128)(4,1)} %bitcast.52), calls=%async_computation.4 | async-start | bytes 8388608
  587.5 14.8 %slice-start.5 = ((s8[12845056]{0:T(1024)(128)(4,1)}), s8[4194304]{0:T(1024)(128)(4,1)S(1)}, s32[]{:S(2)}) async-start(s8[12845056]{0:T(1024)(128)(4,1)} %bitcast.52), calls=%async_computation.5 | async-start | bytes 8388608
  595.8 8.3 %slice-start.6 = ((s8[12845056]{0:T(1024)(128)(4,1)}), s8[4194304]{0:T(1024)(128)(4,1)S(1)}, s32[]{:S(2)}) async-start(s8[12845056]{0:T(1024)(128)(4,1)} %bitcast.52), calls=%async_computation.6 | async-start | bytes 8388608
  595.8 8.3 %slice-start.7 = ((s8[12845056]{0:T(1024)(128)(4,1)}), s8[262144]{0:T(1024)(128)(4,1)S(1)}, s32[]{:S(2)}) async-start(s8[12845056]{0:T(1024)(128)(4,1)} %bitcast.52), calls=%async_computation.7 | async-start | bytes 524288
